TPU v7x, 128 devices: a whole 4x4x4 slice. The times are simulated.
128 devices in a mesh: dp: 32 (over y, x, core), mp: 4 (over z).
Axes of the slice: x: 4, y: 4, z: 4, core: 2. Of those that a mesh axis runs over, the one named last changes fastest.
Arguments:
- hidden_in: bfloat16 [2, 128, 4096], P(None, 'dp', 'mp'), may hold values from -6 to 6
- rec_gain: float32 [2, 4096], replicated, may hold values from 0.5 to 1.5
- rec_in_x: bfloat16 [2, 4096, 4096], P(None, 'dp', 'mp'), may hold values from -0.09375 to 0.09375
- rec_in_y: bfloat16 [2, 4096, 4096], P(None, 'dp', 'mp'), may hold values from -0.09375 to 0.09375
- conv_weight: float32 [2, 4, 4096], P(None, None, 'mp'), may hold values from -3 to 3
- conv_bias: float32 [2, 4096], P(None, 'mp'), may hold values from -3 to 3
- gate_x_weight: bfloat16 [2, 16, 256, 256], P(None, 'mp'), may hold values from -0.375 to 0.375
- gate_x_bias: float32 [2, 4096], P(None, 'mp'), may hold values from -4 to 4
- gate_a_weight: bfloat16 [2, 16, 256, 256], P(None, 'mp'), may hold values from -0.375 to 0.375
- gate_a_bias: float32 [2, 4096], P(None, 'mp'), may hold values from -4 to 4
- decay_param: float32 [2, 4096], P(None, 'mp'), may hold values from -9 to -1
- rec_out: bfloat16 [2, 4096, 4096], P(None, 'dp', 'mp'), may hold values from -0.09375 to 0.09375
- lru_state: bfloat16 [2, 128, 4096], P(None, 'dp', 'mp'), may hold values from -6 to 6
- conv_state: bfloat16 [2, 3, 128, 4096], P(None, None, 'dp', 'mp'), may hold values from -6 to 6
- scale_index: int32 [2], replicated, may hold values from 0 to 7
- attn_gain: float32 [4096], replicated, may hold values from 0.5 to 1.5
- attn_q: bfloat16 [4096, 4096], P('dp', 'mp'), may hold values from -0.09375 to 0.09375
- attn_kv: bfloat16 [4096, 512], P('dp', 'mp'), may hold values from -0.09375 to 0.09375
- attn_out: bfloat16 [4096, 4096], P('dp', 'mp'), may hold values from -0.09375 to 0.09375
- key_cache: bfloat16 [128, 2048, 256], P('dp', 'mp'), may hold values from -400 to 400
- value_cache: bfloat16 [128, 2048, 256], P('dp', 'mp'), may hold values from -6 to 6
- positions: int32 [128], P('dp'), may hold values from 1 to 6143
Outputs:
- hidden_out: bfloat16 [2, 128, 4096], P(None, 'dp', 'mp')
- lru_out: bfloat16 [2, 128, 4096], P(None, 'dp', 'mp')
- conv_out: bfloat16 [2, 3, 128, 4096], P(None, None, 'dp', 'mp')
- new_kv: bfloat16 [2, 128, 512], P(None, 'dp', 'mp')
Inputs may be any that keep to these rules, and one draw needn't show every extreme that they name: `positions`: the count of tokens a sequence has seen; the cache holds its last min(that count, 2048) tokens.
All inputs are finite; a program needn't handle non-finite values.
Results may differ from a plain program's by a relative error of at most 0.03.
Values may be sent and summed in bfloat16 or wider, within the bound.
A program may use at most 64 MiB of HBM per device.

v0:
```python
import jax
import jax.numpy as jnp
from jax import lax
from jax.sharding import PartitionSpec as P

HEADS = 16
HEAD_DIM = 256
WIN = 2048
LAYERS = 2
STEPS = 2


def cut_along(array, dim, devices):
    lengths = array.shape
    pieces = array.reshape(*lengths[:dim], devices, lengths[dim] // devices, *lengths[dim + 1 :])
    return jnp.moveaxis(pieces, dim, 0)


def sent_and_summed(array, axis, dim):
    devices = lax.axis_size(axis)
    pieces = lax.all_to_all(cut_along(array, dim, devices), axis, 0, 0, tiled=True)
    return jnp.sum(pieces, axis=0)


def from_everyone(array, axis):
    copies = jnp.broadcast_to(array, (lax.axis_size(axis), *array.shape))
    return lax.all_to_all(copies, axis, split_axis=0, concat_axis=0, tiled=True)


def joined_along(pieces, dim):
    pieces = jnp.moveaxis(pieces, 0, dim)
    lengths = pieces.shape
    return pieces.reshape(*lengths[:dim], lengths[dim] * lengths[dim + 1], *lengths[dim + 2 :])


def gathered_copies(array, axis, dim):
    pieces = from_everyone(array, axis)
    return joined_along(pieces, dim)


def all_in_one(array, axis):
    leaves = jax.tree.leaves(array)
    sequence = sorted(range(len(leaves)), key=lambda k: -leaves[k].size)
    width = (1, *leaves[sequence[0]].shape)[-1]
    lines = [
        jnp.pad(leaves[k].reshape(-1), (0, -leaves[k].size % width)).reshape(-1, width)
        for k in sequence
    ]
    both, at, found = (from_everyone(jnp.concatenate(lines), axis), 0, {})
    for k, line in zip(sequence, lines):
        share = both[:, at : at + len(line)].reshape(len(both), -1)
        found[k] = share[:, : leaves[k].size].reshape(-1, *leaves[k].shape)
        at += len(line)
    numbers = iter(range(len(leaves)))
    return jax.tree.map(lambda _: found[next(numbers)], array)


def joined_by_halves(pieces, combine):
    while len(jax.tree.leaves(pieces)[0]) > 1:
        pieces = jax.vmap(combine)(
            *(jax.tree.map(lambda part: part[side::2], pieces) for side in (0, 1))
        )
    return jax.tree.map(lambda part: part[0], pieces)


def joined_all(array, axis, combine):
    pieces = all_in_one(
        jax.tree.map(
            lambda part, kind: part.astype(kind), array, (jnp.bfloat16, jnp.bfloat16, jnp.bfloat16)
        ),
        axis,
    )
    return joined_by_halves(
        jax.tree.map(lambda part, own: part.astype(own.dtype), pieces, array), combine
    )


def norm_rows(values, gain):
    mean_sq = jnp.mean(values * values, axis=-1, keepdims=True)
    return (values * lax.rsqrt(mean_sq + 1e-06) * gain).astype(jnp.bfloat16)


def spread_project(normed, weight):
    spread = lax.all_to_all(normed, "dp", split_axis=1, concat_axis=0, tiled=True)
    return sent_and_summed(jnp.dot(spread, weight, preferred_element_type=jnp.float32), "dp", 0)


def full_stream(stream):
    return gathered_copies(stream, "mp", 1)


def full_features(values):
    return gathered_copies(values, "mp", 1)


def lru_gate(filtered_half, weight, bias):
    rows = filtered_half.shape[0]
    shaped = filtered_half.reshape(rows, weight.shape[0], weight.shape[1])
    mixed = jnp.einsum("bhi,hij->bhj", shaped, weight, preferred_element_type=jnp.float32)
    return jax.nn.sigmoid(mixed.reshape(rows, -1) + bias)


def combine(first, second):
    top_first, total_first, summed_first = first
    top_second, total_second, summed_second = second
    best = jnp.maximum(top_first, top_second)
    fade_first = jnp.exp(top_first - best)
    fade_second = jnp.exp(top_second - best)
    total = total_first * fade_first + total_second * fade_second
    summed = summed_first * fade_first[..., None] + summed_second * fade_second[..., None]
    return (best, total, summed)


def recurrent_layer(
    stream,
    gain,
    in_x,
    in_y,
    conv_taps,
    conv_shift,
    gx_weight,
    gx_bias,
    ga_weight,
    ga_bias,
    decay,
    out_weight,
    state,
    window,
):
    normed = norm_rows(full_stream(stream), gain)
    width = in_x.shape[1]
    both = spread_project(normed, jnp.concatenate([in_x, in_y], axis=1))
    branch_input = both[:, :width]
    branch_gate = both[:, width:]
    driven = branch_input.astype(jnp.bfloat16)
    gating = jax.nn.gelu(branch_gate, approximate=True)
    taps = jnp.concatenate([window, driven[None]], 0)
    filtered = jnp.sum(taps.astype(jnp.float32) * conv_taps[:, None, :], axis=0) + conv_shift
    filtered_half = filtered.astype(jnp.bfloat16)
    input_gate = lru_gate(filtered_half, gx_weight, gx_bias)
    decay_gate = lru_gate(filtered_half, ga_weight, ga_bias)
    log_decay = -8.0 * decay_gate * jax.nn.softplus(decay)
    state = jnp.exp(log_decay) * state + jnp.sqrt(1.0 - jnp.exp(2.0 * log_decay)) * (
        input_gate * filtered
    )
    mixed = (state * gating).astype(jnp.bfloat16)
    stream = stream + spread_project(full_features(mixed), out_weight)
    return (stream, state, taps[1:])


def attention_layer(
    stream,
    gain,
    w_query,
    w_keyvalue,
    w_out,
    key_cache,
    value_cache,
    positions,
    fresh_keys,
    fresh_values,
    step,
):
    normed = norm_rows(full_stream(stream), gain)
    query_cols = w_query.shape[1]
    local = spread_project(normed, jnp.concatenate([w_query, w_keyvalue], axis=1)).astype(
        jnp.bfloat16
    )
    kv_local = local[:, query_cols:]
    rows = local.shape[0]
    groups = full_features(local).reshape(rows, -1, local.shape[1])
    query = groups[:, :, :query_cols].reshape(rows, HEADS, HEAD_DIM)
    key_value = groups[:, :, query_cols:].reshape(rows, 2 * HEAD_DIM)
    fresh_keys.append(key_value[:, :HEAD_DIM])
    fresh_values.append(key_value[:, HEAD_DIM:])
    slots = key_cache.shape[1]
    slot_ids = lax.axis_index("mp") * slots + jnp.arange(slots, dtype=jnp.int32)
    position = positions[:, None]
    held = position - 1 - jnp.mod(position - 1 - slot_ids[None, :], WIN)
    valid = ((held >= 0) & (held >= position + step - WIN + 1))[:, None, :]
    scores = jnp.einsum(
        "bhd,bsd->bhs", query, key_cache, preferred_element_type=jnp.float32
    ) * HEAD_DIM ** (-0.5)
    masked = jnp.where(valid, scores, -1e30)
    top = jnp.max(masked, axis=-1)
    weights = jnp.where(valid, jnp.exp(masked - top[..., None]), 0.0)
    total = jnp.sum(weights, axis=-1)
    summed = jnp.einsum(
        "bhs,bsd->bhd",
        weights.astype(jnp.bfloat16),
        value_cache,
        preferred_element_type=jnp.float32,
    )
    top, total, summed = joined_all((top, total, summed), "mp", combine)
    new_keys = jnp.stack(fresh_keys, 1)
    new_values = jnp.stack(fresh_values, 1)
    fresh_scores = jnp.einsum(
        "bhd,bnd->bhn", query, new_keys, preferred_element_type=jnp.float32
    ) * HEAD_DIM ** (-0.5)
    best = jnp.maximum(top, jnp.max(fresh_scores, axis=-1))
    fade = jnp.exp(top - best)
    fresh_weights = jnp.exp(fresh_scores - best[..., None])
    total = total * fade + jnp.sum(fresh_weights, axis=-1)
    summed = summed * fade[..., None] + jnp.einsum(
        "bhn,bnd->bhd",
        fresh_weights.astype(jnp.bfloat16),
        new_values,
        preferred_element_type=jnp.float32,
    )
    attended = (summed / total[..., None]).astype(jnp.bfloat16).reshape(rows, HEADS * HEAD_DIM)
    stream = stream + spread_project(attended, w_out)
    return (stream, kv_local)


def body(
    hidden_in,
    rec_gain,
    rec_in_x,
    rec_in_y,
    conv_weight,
    conv_bias,
    gate_x_weight,
    gate_x_bias,
    gate_a_weight,
    gate_a_bias,
    decay_param,
    rec_out,
    lru_state,
    conv_state,
    scale_index,
    attn_gain,
    attn_q,
    attn_kv,
    attn_out,
    key_cache,
    value_cache,
    positions,
):
    scales = 2.0 ** ((scale_index.astype(jnp.float32) - 4.0) * 0.5)
    states = [lru_state[layer].astype(jnp.float32) * scales[layer] for layer in range(LAYERS)]
    windows = [conv_state[layer] for layer in range(LAYERS)]
    fresh_keys = []
    fresh_values = []
    outputs = []
    kv_parts = []
    for step in range(STEPS):
        stream = hidden_in[step].astype(jnp.float32)
        for layer in range(LAYERS):
            stream, states[layer], windows[layer] = recurrent_layer(
                stream,
                rec_gain[layer],
                rec_in_x[layer],
                rec_in_y[layer],
                conv_weight[layer],
                conv_bias[layer],
                gate_x_weight[layer],
                gate_x_bias[layer],
                gate_a_weight[layer],
                gate_a_bias[layer],
                decay_param[layer],
                rec_out[layer],
                states[layer],
                windows[layer],
            )
        stream, kv_local = attention_layer(
            stream,
            attn_gain,
            attn_q,
            attn_kv,
            attn_out,
            key_cache,
            value_cache,
            positions,
            fresh_keys,
            fresh_values,
            step,
        )
        kv_parts.append(kv_local)
        outputs.append(stream.astype(jnp.bfloat16))
    lru_new = jnp.stack(
        [(states[layer] / scales[layer]).astype(jnp.bfloat16) for layer in range(LAYERS)], 0
    )
    return (jnp.stack(outputs, 0), lru_new, jnp.stack(windows, 0), jnp.stack(kv_parts, 0))


def solution(mesh):
    placed = (
        P(None, "dp", "mp"),
        P(),
        P(None, "dp", "mp"),
        P(None, "dp", "mp"),
        P(None, None, "mp"),
        P(None, "mp"),
        P(None, "mp", None, None),
        P(None, "mp"),
        P(None, "mp", None, None),
        P(None, "mp"),
        P(None, "mp"),
        P(None, "dp", "mp"),
        P(None, "dp", "mp"),
        P(None, None, "dp", "mp"),
        P(),
        P(),
        P("dp", "mp"),
        P("dp", "mp"),
        P("dp", "mp"),
        P("dp", "mp", None),
        P("dp", "mp", None),
        P("dp"),
    )
    return jax.shard_map(
        body,
        mesh=mesh,
        in_specs=placed,
        out_specs=(
            P(None, "dp", "mp"),
            P(None, "dp", "mp"),
            P(None, None, "dp", "mp"),
            P(None, "dp", "mp"),
        ),
        check_vma=False,
    )
```

profile of v0, /device:TPU:0, one launch (start us, length us, event | category | flops | bytes accessed | tf_op | source)
XLA Modules:
  0.0 500.4 jit_solution(3061832150655396843)
XLA Ops:
  2.1 5.4 %all-to-all-start.19 = ((f32[4,4,1024]{2,1,0:T(4,128)}), f32[4,4,1024]{2,1,0:T(4,128)S(1)}, u32[]{:S(2)}, u32[]{:S(2)}) async-start(f32[4,4,1024]{2,1,0:T(4,128)} %broadcast_in_dim.128), calls=%async_computation.19 | async-start | bytes 131072 | tf_op jit(solution)/shard_map/all_to_all | solution.py:27
  17.2 5.4 %all-to-all-done = f32[4,4,1024]{2,1,0:T(4,128)S(1)} async-done(((f32[4,4,1024]{2,1,0:T(4,128)}), f32[4,4,1024]{2,1,0:T(4,128)S(1)}, u32[]{:S(2)}, u32[]{:S(2)}) %all-to-all-start) | async-done | bytes 65568 | tf_op jit(solution)/shard_map/all_to_all | solution.py:27
  23.6 7.3 %all-to-all-start.1 = ((bf16[4,32,128]{2,0,1:T(4,128)(2,1)}), bf16[4,32,128]{2,0,1:T(4,128)(2,1)S(1)}, u32[]{:S(2)}, u32[]{:S(2)}) async-start(bf16[4,32,128]{2,0,1:T(4,128)(2,1)} %get-tuple-element.48), calls=%async_computation.1 | async-start | bytes 65536 | tf_op jit(solution)/shard_map/all_to_all | solution.py:84
  32.7 5.6 %all-to-all-done.1 = bf16[4,32,128]{2,0,1:T(4,128)(2,1)S(1)} async-done(((bf16[4,32,128]{2,0,1:T(4,128)(2,1)}), bf16[4,32,128]{2,0,1:T(4,128)(2,1)S(1)}, u32[]{:S(2)}, u32[]{:S(2)}) %all-to-all-start.1) | async-done | bytes 32800 | tf_op jit(solution)/shard_map/all_to_all | solution.py:84
  44.0 5.5 %all-to-all-done.20 = bf16[4,32,128]{2,0,1:T(4,128)(2,1)S(1)} async-done(((bf16[4,32,128]{2,0,1:T(4,128)(2,1)}), bf16[4,32,128]{2,0,1:T(4,128)(2,1)S(1)}, u32[]{:S(2)}, u32[]{:S(2)}) %all-to-all-start.20) | async-done | bytes 32800 | tf_op jit(solution)/shard_map/all_to_all | solution.py:84
  59.0 11.7 %all-to-all-done.2 = f32[32,4,2048]{2,1,0:T(4,128)S(1)} async-done(((f32[32,4,2048]{2,1,0:T(4,128)}), f32[32,4,2048]{2,1,0:T(4,128)S(1)}, u32[]{:S(2)}, u32[]{:S(2)}) %all-to-all-start.2) | async-done | bytes 1048608 | tf_op jit(solution)/shard_map/all_to_all | solution.py:21
  78.1 14.5 %all-to-all-done.21 = f32[32,4,2048]{2,1,0:T(4,128)} async-done(((f32[32,4,2048]{2,1,0:T(4,128)}), f32[32,4,2048]{2,1,0:T(4,128)}, u32[]{:S(2)}, u32[]{:S(2)}) %all-to-all-start.21) | async-done | bytes 1048608 | tf_op jit(solution)/shard_map/all_to_all | solution.py:21
  97.8 7.8 %all_to_all.304 = bf16[4,4,1024]{2,1,0:T(4,128)(2,1)S(1)} all-to-all(bf16[4,4,1024]{2,1,0:T(4,128)(2,1)S(1)} %broadcast_in_dim.130), channel_id=1, replica_groups=mesh['dp'=32,'mp'=4] {'mp'}, dimensions={0} | all-to-all | bytes 65536 | tf_op jit(solution)/shard_map/all_to_all | solution.py:27
  105.6 8.5 %all_to_all.305 = bf16[4,4,1024]{2,1,0:T(4,128)(2,1)} all-to-all(bf16[4,4,1024]{2,1,0:T(4,128)(2,1)S(1)} %broadcast_in_dim.118), channel_id=1, replica_groups=mesh['dp'=32,'mp'=4] {'mp'}, dimensions={0} | all-to-all | bytes 65536 | tf_op jit(solution)/shard_map/all_to_all | solution.py:27
  114.1 10.8 %all_to_all.306 = bf16[4,32,128]{2,0,1:T(4,128)(2,1)S(1)} all-to-all(bf16[4,32,128]{2,0,1:T(4,128)(2,1)S(1)} %bitcast.416), channel_id=1, replica_groups=mesh['dp'=32,'mp'=4] {'dp'}, dimensions={1} | all-to-all | bytes 65536 | tf_op jit(solution)/shard_map/all_to_all | solution.py:84
  143.1 9.3 %all-to-all-done.24 = f32[32,4,1024]{2,1,0:T(4,128)} async-done(((f32[32,4,1024]{2,1,0:T(4,128)}), f32[32,4,1024]{2,1,0:T(4,128)}, u32[]{:S(2)}, u32[]{:S(2)}) %all-to-all-start.24) | async-done | bytes 524320 | tf_op jit(solution)/shard_map/all_to_all | solution.py:21
  158.1 10.4 %all-to-all-done.5 = f32[32,4,1024]{2,1,0:T(4,128)} async-done(((f32[32,4,1024]{2,1,0:T(4,128)}), f32[32,4,1024]{2,1,0:T(4,128)}, u32[]{:S(2)}, u32[]{:S(2)}) %all-to-all-start.5) | async-done | bytes 524320 | tf_op jit(solution)/shard_map/all_to_all | solution.py:21
  170.9 8.0 %all_to_all.307 = f32[4,4,1024]{2,1,0:T(4,128)S(1)} all-to-all(f32[4,4,1024]{2,1,0:T(4,128)S(1)} %broadcast_in_dim.131), channel_id=1, replica_groups=mesh['dp'=32,'mp'=4] {'mp'}, dimensions={0} | all-to-all | bytes 131072 | tf_op jit(solution)/shard_map/all_to_all | solution.py:27
  190.0 10.9 %all_to_all.308 = bf16[4,32,128]{2,0,1:T(4,128)(2,1)S(1)} all-to-all(bf16[4,32,128]{2,0,1:T(4,128)(2,1)S(1)} %get-tuple-element.45), channel_id=1, replica_groups=mesh['dp'=32,'mp'=4] {'dp'}, dimensions={1} | all-to-all | bytes 65536 | tf_op jit(solution)/shard_map/all_to_all | solution.py:84
  219.8 14.1 %all-to-all-done.27 = f32[32,4,2048]{2,1,0:T(4,128)} async-done(((f32[32,4,2048]{2,1,0:T(4,128)}), f32[32,4,2048]{2,1,0:T(4,128)}, u32[]{:S(2)}, u32[]{:S(2)}) %all-to-all-start.27) | async-done | bytes 1048608 | tf_op jit(solution)/shard_map/all_to_all | solution.py:21
  240.8 15.2 %all-to-all-done.8 = f32[32,4,2048]{2,1,0:T(4,128)} async-done(((f32[32,4,2048]{2,1,0:T(4,128)}), f32[32,4,2048]{2,1,0:T(4,128)}, u32[]{:S(2)}, u32[]{:S(2)}) %all-to-all-start.8) | async-done | bytes 1048608 | tf_op jit(solution)/shard_map/all_to_all | solution.py:21
  260.5 7.8 %all_to_all.309 = bf16[4,4,1024]{2,1,0:T(4,128)(2,1)S(1)} all-to-all(bf16[4,4,1024]{2,1,0:T(4,128)(2,1)S(1)} %broadcast_in_dim.133), channel_id=1, replica_groups=mesh['dp'=32,'mp'=4] {'mp'}, dimensions={0} | all-to-all | bytes 65536 | tf_op jit(solution)/shard_map/all_to_all | solution.py:27
  268.3 8.5 %all_to_all.310 = bf16[4,4,1024]{2,1,0:T(4,128)(2,1)} all-to-all(bf16[4,4,1024]{2,1,0:T(4,128)(2,1)S(1)} %broadcast_in_dim.121), channel_id=1, replica_groups=mesh['dp'=32,'mp'=4] {'mp'}, dimensions={0} | all-to-all | bytes 65536 | tf_op jit(solution)/shard_map/all_to_all | solution.py:27
  276.8 10.8 %all_to_all.311 = bf16[4,32,128]{2,0,1:T(4,128)(2,1)S(1)} all-to-all(bf16[4,32,128]{2,0,1:T(4,128)(2,1)S(1)} %bitcast.417), channel_id=1, replica_groups=mesh['dp'=32,'mp'=4] {'dp'}, dimensions={1} | all-to-all | bytes 65536 | tf_op jit(solution)/shard_map/all_to_all | solution.py:84
  292.9 6.0 %all-to-all-done.10 = bf16[4,32,128]{2,0,1:T(4,128)(2,1)S(1)} async-done(((bf16[4,32,128]{2,0,1:T(4,128)(2,1)}), bf16[4,32,128]{2,0,1:T(4,128)(2,1)S(1)}, u32[]{:S(2)}, u32[]{:S(2)}) %all-to-all-start.10) | async-done | bytes 32800 | tf_op jit(solution)/shard_map/all_to_all | solution.py:84
  304.1 10.2 %all-to-all-done.30 = f32[32,4,1024]{2,1,0:T(4,128)S(1)} async-done(((f32[32,4,1024]{2,1,0:T(4,128)}), f32[32,4,1024]{2,1,0:T(4,128)S(1)}, u32[]{:S(2)}, u32[]{:S(2)}) %all-to-all-start.30) | async-done | bytes 524320 | tf_op jit(solution)/shard_map/all_to_all | solution.py:21
  319.0 10.9 %all-to-all-done.11 = f32[32,4,1024]{2,1,0:T(4,128)S(1)} async-done(((f32[32,4,1024]{2,1,0:T(4,128)}), f32[32,4,1024]{2,1,0:T(4,128)S(1)}, u32[]{:S(2)}, u32[]{:S(2)}) %all-to-all-start.11) | async-done | bytes 524320 | tf_op jit(solution)/shard_map/all_to_all | solution.py:21
  343.5 5.4 %all-to-all-done.12 = f32[4,4,1024]{2,1,0:T(4,128)S(1)} async-done(((f32[4,4,1024]{2,1,0:T(4,128)}), f32[4,4,1024]{2,1,0:T(4,128)S(1)}, u32[]{:S(2)}, u32[]{:S(2)}) %all-to-all-start.12) | async-done | bytes 65568 | tf_op jit(solution)/shard_map/all_to_all | solution.py:27
  349.8 10.9 %all_to_all.312 = bf16[4,32,128]{2,0,1:T(4,128)(2,1)S(1)} all-to-all(bf16[4,32,128]{2,0,1:T(4,128)(2,1)S(1)} %get-tuple-element.43), channel_id=1, replica_groups=mesh['dp'=32,'mp'=4] {'dp'}, dimensions={1} | all-to-all | bytes 65536 | tf_op jit(solution)/shard_map/all_to_all | solution.py:84
  366.1 6.0 %all-to-all-done.13 = bf16[4,32,128]{2,0,1:T(4,128)(2,1)S(1)} async-done(((bf16[4,32,128]{2,0,1:T(4,128)(2,1)}), bf16[4,32,128]{2,0,1:T(4,128)(2,1)S(1)}, u32[]{:S(2)}, u32[]{:S(2)}) %all-to-all-start.13) | async-done | bytes 32800 | tf_op jit(solution)/shard_map/all_to_all | solution.py:84
  378.1 10.2 %all-to-all-done.33 = f32[32,4,1152]{2,1,0:T(4,128)S(1)} async-done(((f32[32,4,1152]{2,1,0:T(4,128)}), f32[32,4,1152]{2,1,0:T(4,128)S(1)}, u32[]{:S(2)}, u32[]{:S(2)}) %all-to-all-start.33) | async-done | bytes 589856 | tf_op jit(solution)/shard_map/all_to_all | solution.py:21
  394.6 10.0 %all-to-all-done.14 = f32[32,4,1152]{2,1,0:T(4,128)S(1)} async-done(((f32[32,4,1152]{2,1,0:T(4,128)}), f32[32,4,1152]{2,1,0:T(4,128)S(1)}, u32[]{:S(2)}, u32[]{:S(2)}) %all-to-all-start.14) | async-done | bytes 589856 | tf_op jit(solution)/shard_map/all_to_all | solution.py:21
  430.4 5.5 %all-to-all-done.35 = bf16[4,66,256]{2,1,0:T(8,128)(2,1)S(1)} async-done(((bf16[4,66,256]{2,1,0:T(8,128)(2,1)}), bf16[4,66,256]{2,1,0:T(8,128)(2,1)S(1)}, u32[]{:S(2)}, u32[]{:S(2)}) %all-to-all-start.35) | async-done | bytes 135200 | tf_op jit(solution)/shard_map/all_to_all | solution.py:27
  451.2 6.2 %all-to-all-done.36 = bf16[4,32,128]{2,0,1:T(4,128)(2,1)S(1)} async-done(((bf16[4,32,128]{2,0,1:T(4,128)(2,1)}), bf16[4,32,128]{2,0,1:T(4,128)(2,1)S(1)}, u32[]{:S(2)}, u32[]{:S(2)}) %all-to-all-start.36) | async-done | bytes 32800 | tf_op jit(solution)/shard_map/all_to_all | solution.py:84
  462.6 6.0 %all-to-all-done.17 = bf16[4,32,128]{2,0,1:T(4,128)(2,1)S(1)} async-done(((bf16[4,32,128]{2,0,1:T(4,128)(2,1)}), bf16[4,32,128]{2,0,1:T(4,128)(2,1)S(1)}, u32[]{:S(2)}, u32[]{:S(2)}) %all-to-all-start.17) | async-done | bytes 32800 | tf_op jit(solution)/shard_map/all_to_all | solution.py:84
  475.3 8.8 %all-to-all-done.37 = f32[32,4,1024]{2,1,0:T(4,128)S(1)} async-done(((f32[32,4,1024]{2,1,0:T(4,128)}), f32[32,4,1024]{2,1,0:T(4,128)S(1)}, u32[]{:S(2)}, u32[]{:S(2)}) %all-to-all-start.37) | async-done | bytes 524320 | tf_op jit(solution)/shard_map/all_to_all | solution.py:21
  488.7 10.9 %all-to-all-done.18 = f32[32,4,1024]{2,1,0:T(4,128)S(1)} async-done(((f32[32,4,1024]{2,1,0:T(4,128)}), f32[32,4,1024]{2,1,0:T(4,128)S(1)}, u32[]{:S(2)}, u32[]{:S(2)}) %all-to-all-start.18) | async-done | bytes 524320 | tf_op jit(solution)/shard_map/all_to_all | solution.py:21
  (390 shorter events, 214.0 us)
Async XLA Ops:
  0.6 422.9 %copy-start = (bf16[4,512,256]{2,1,0:T(8,128)(2,1)S(1)}, bf16[4,512,256]{2,1,0:T(8,128)(2,1)}, u32[]{:S(2)}) copy-start(bf16[4,512,256]{2,1,0:T(8,128)(2,1)} %param.41) | copy-start | bytes 3145732
  2.1 11.0 %all-to-all-start.19 = ((f32[4,4,1024]{2,1,0:T(4,128)}), f32[4,4,1024]{2,1,0:T(4,128)S(1)}, u32[]{:S(2)}, u32[]{:S(2)}) async-start(f32[4,4,1024]{2,1,0:T(4,128)} %broadcast_in_dim.128), calls=%async_computation.19 | async-start | bytes 131072 | tf_op jit(solution)/shard_map/all_to_all | solution.py:27
  13.8 8.9 %all-to-all-start = ((f32[4,4,1024]{2,1,0:T(4,128)}), f32[4,4,1024]{2,1,0:T(4,128)S(1)}, u32[]{:S(2)}, u32[]{:S(2)}) async-start(f32[4,4,1024]{2,1,0:T(4,128)} %broadcast_in_dim.116), calls=%async_computation | async-start | bytes 131072 | tf_op jit(solution)/shard_map/all_to_all | solution.py:27
  23.6 14.7 %all-to-all-start.1 = ((bf16[4,32,128]{2,0,1:T(4,128)(2,1)}), bf16[4,32,128]{2,0,1:T(4,128)(2,1)S(1)}, u32[]{:S(2)}, u32[]{:S(2)}) async-start(bf16[4,32,128]{2,0,1:T(4,128)(2,1)} %get-tuple-element.48), calls=%async_computation.1 | async-start | bytes 65536 | tf_op jit(solution)/shard_map/all_to_all | solution.py:84
  38.3 11.2 %all-to-all-start.20 = ((bf16[4,32,128]{2,0,1:T(4,128)(2,1)}), bf16[4,32,128]{2,0,1:T(4,128)(2,1)S(1)}, u32[]{:S(2)}, u32[]{:S(2)}) async-start(bf16[4,32,128]{2,0,1:T(4,128)(2,1)} %get-tuple-element.49), calls=%async_computation.20 | async-start | bytes 65536 | tf_op jit(solution)/shard_map/all_to_all | solution.py:84
  49.5 21.1 %all-to-all-start.2 = ((f32[32,4,2048]{2,1,0:T(4,128)}), f32[32,4,2048]{2,1,0:T(4,128)S(1)}, u32[]{:S(2)}, u32[]{:S(2)}) async-start(f32[32,4,2048]{2,1,0:T(4,128)} %copy.95), calls=%async_computation.2 | async-start | bytes 2097152 | tf_op jit(solution)/shard_map/all_to_all | solution.py:21
  54.6 43.0 %copy-start.61 = (f32[1,1024]{1,0:T(1,128)}, f32[1,1024]{1,0:T(1,128)S(1)}, u32[]{:S(2)}) copy-start(f32[1,1024]{1,0:T(1,128)S(1)} %get-tuple-element.59) | copy-start | bytes 12292
  70.6 22.0 %all-to-all-start.21 = ((f32[32,4,2048]{2,1,0:T(4,128)}), f32[32,4,2048]{2,1,0:T(4,128)}, u32[]{:S(2)}, u32[]{:S(2)}) async-start(f32[32,4,2048]{2,1,0:T(4,128)} %copy.111), calls=%async_computation.21 | async-start | bytes 2097152 | tf_op jit(solution)/shard_map/all_to_all | solution.py:21
  124.9 11.3 %all-to-all-start.4 = ((bf16[4,32,128]{2,0,1:T(4,128)(2,1)}), bf16[4,32,128]{2,0,1:T(4,128)(2,1)S(1)}, u32[]{:S(2)}, u32[]{:S(2)}) async-start(bf16[4,32,128]{2,0,1:T(4,128)(2,1)} %bitcast.25), calls=%async_computation.4 | async-start | bytes 65536 | tf_op jit(solution)/shard_map/all_to_all | solution.py:84
  136.2 16.2 %all-to-all-start.24 = ((f32[32,4,1024]{2,1,0:T(4,128)}), f32[32,4,1024]{2,1,0:T(4,128)}, u32[]{:S(2)}, u32[]{:S(2)}) async-start(f32[32,4,1024]{2,1,0:T(4,128)} %copy.114), calls=%async_computation.24 | async-start | bytes 1048576 | tf_op jit(solution)/shard_map/all_to_all | solution.py:21
  152.4 16.2 %all-to-all-start.5 = ((f32[32,4,1024]{2,1,0:T(4,128)}), f32[32,4,1024]{2,1,0:T(4,128)}, u32[]{:S(2)}, u32[]{:S(2)}) async-start(f32[32,4,1024]{2,1,0:T(4,128)} %copy.98), calls=%async_computation.5 | async-start | bytes 1048576 | tf_op jit(solution)/shard_map/all_to_all | solution.py:21
  179.5 8.9 %all-to-all-start.6 = ((f32[4,4,1024]{2,1,0:T(4,128)}), f32[4,4,1024]{2,1,0:T(4,128)S(1)}, u32[]{:S(2)}, u32[]{:S(2)}) async-start(f32[4,4,1024]{2,1,0:T(4,128)} %broadcast_in_dim.119), calls=%async_computation.6 | async-start | bytes 131072 | tf_op jit(solution)/shard_map/all_to_all | solution.py:27
  200.8 11.3 %all-to-all-start.7 = ((bf16[4,32,128]{2,0,1:T(4,128)(2,1)}), bf16[4,32,128]{2,0,1:T(4,128)(2,1)S(1)}, u32[]{:S(2)}, u32[]{:S(2)}) async-start(bf16[4,32,128]{2,0,1:T(4,128)(2,1)} %get-tuple-element.44), calls=%async_computation.7 | async-start | bytes 65536 | tf_op jit(solution)/shard_map/all_to_all | solution.py:84
  212.1 21.9 %all-to-all-start.27 = ((f32[32,4,2048]{2,1,0:T(4,128)}), f32[32,4,2048]{2,1,0:T(4,128)}, u32[]{:S(2)}, u32[]{:S(2)}) async-start(f32[32,4,2048]{2,1,0:T(4,128)} %copy.116), calls=%async_computation.27 | async-start | bytes 2097152 | tf_op jit(solution)/shard_map/all_to_all | solution.py:21
  234.0 22.0 %all-to-all-start.8 = ((f32[32,4,2048]{2,1,0:T(4,128)}), f32[32,4,2048]{2,1,0:T(4,128)}, u32[]{:S(2)}, u32[]{:S(2)}) async-start(f32[32,4,2048]{2,1,0:T(4,128)} %copy.100), calls=%async_computation.8 | async-start | bytes 2097152 | tf_op jit(solution)/shard_map/all_to_all | solution.py:21
  258.7 32.7 %copy-start.6 = (bf16[2,128,1024]{2,1,0:T(8,128)(2,1)S(1)}, bf16[2,128,1024]{2,1,0:T(8,128)(2,1)}, u32[]{:S(2)}) copy-start(bf16[2,128,1024]{2,1,0:T(8,128)(2,1)} %param.33) | copy-start | bytes 1572868
  287.6 11.3 %all-to-all-start.10 = ((bf16[4,32,128]{2,0,1:T(4,128)(2,1)}), bf16[4,32,128]{2,0,1:T(4,128)(2,1)S(1)}, u32[]{:S(2)}, u32[]{:S(2)}) async-start(bf16[4,32,128]{2,0,1:T(4,128)(2,1)} %bitcast.54), calls=%async_computation.10 | async-start | bytes 65536 | tf_op jit(solution)/shard_map/all_to_all | solution.py:84
  298.9 15.5 %all-to-all-start.30 = ((f32[32,4,1024]{2,1,0:T(4,128)}), f32[32,4,1024]{2,1,0:T(4,128)S(1)}, u32[]{:S(2)}, u32[]{:S(2)}) async-start(f32[32,4,1024]{2,1,0:T(4,128)} %copy.119), calls=%async_computation.30 | async-start | bytes 1048576 | tf_op jit(solution)/shard_map/all_to_all | solution.py:21
  314.4 15.5 %all-to-all-start.11 = ((f32[32,4,1024]{2,1,0:T(4,128)}), f32[32,4,1024]{2,1,0:T(4,128)S(1)}, u32[]{:S(2)}, u32[]{:S(2)}) async-start(f32[32,4,1024]{2,1,0:T(4,128)} %copy.103), calls=%async_computation.11 | async-start | bytes 1048576 | tf_op jit(solution)/shard_map/all_to_all | solution.py:21
  330.5 8.9 %all-to-all-start.31 = ((f32[4,4,1024]{2,1,0:T(4,128)}), f32[4,4,1024]{2,1,0:T(4,128)S(1)}, u32[]{:S(2)}, u32[]{:S(2)}) async-start(f32[4,4,1024]{2,1,0:T(4,128)} %broadcast_in_dim.135), calls=%async_computation.31 | async-start | bytes 131072 | tf_op jit(solution)/shard_map/all_to_all | solution.py:27
  340.0 8.9 %all-to-all-start.12 = ((f32[4,4,1024]{2,1,0:T(4,128)}), f32[4,4,1024]{2,1,0:T(4,128)S(1)}, u32[]{:S(2)}, u32[]{:S(2)}) async-start(f32[4,4,1024]{2,1,0:T(4,128)} %broadcast_in_dim.123), calls=%async_computation.12 | async-start | bytes 131072 | tf_op jit(solution)/shard_map/all_to_all | solution.py:27
  360.6 11.4 %all-to-all-start.13 = ((bf16[4,32,128]{2,0,1:T(4,128)(2,1)}), bf16[4,32,128]{2,0,1:T(4,128)(2,1)S(1)}, u32[]{:S(2)}, u32[]{:S(2)}) async-start(bf16[4,32,128]{2,0,1:T(4,128)(2,1)} %get-tuple-element.42), calls=%async_computation.13 | async-start | bytes 65536 | tf_op jit(solution)/shard_map/all_to_all | solution.py:84
  372.0 16.2 %all-to-all-start.33 = ((f32[32,4,1152]{2,1,0:T(4,128)}), f32[32,4,1152]{2,1,0:T(4,128)S(1)}, u32[]{:S(2)}, u32[]{:S(2)}) async-start(f32[32,4,1152]{2,1,0:T(4,128)} %copy.121), calls=%async_computation.33 | async-start | bytes 1179648 | tf_op jit(solution)/shard_map/all_to_all | solution.py:21
  388.3 16.3 %all-to-all-start.14 = ((f32[32,4,1152]{2,1,0:T(4,128)}), f32[32,4,1152]{2,1,0:T(4,128)S(1)}, u32[]{:S(2)}, u32[]{:S(2)}) async-start(f32[32,4,1152]{2,1,0:T(4,128)} %copy.105), calls=%async_computation.14 | async-start | bytes 1179648 | tf_op jit(solution)/shard_map/all_to_all | solution.py:21
  405.3 8.9 %all-to-all-start.34 = ((bf16[4,4,1152]{2,1,0:T(4,128)(2,1)}), bf16[4,4,1152]{2,1,0:T(4,128)(2,1)S(1)}, u32[]{:S(2)}, u32[]{:S(2)}) async-start(bf16[4,4,1152]{2,1,0:T(4,128)(2,1)} %broadcast_in_dim.136), calls=%async_computation.34 | async-start | bytes 73728 | tf_op jit(solution)/shard_map/all_to_all | solution.py:27
  414.8 8.7 %all-to-all-start.15 = ((bf16[4,4,1152]{2,1,0:T(4,128)(2,1)}), bf16[4,4,1152]{2,1,0:T(4,128)(2,1)S(1)}, u32[]{:S(2)}, u32[]{:S(2)}) async-start(bf16[4,4,1152]{2,1,0:T(4,128)(2,1)} %broadcast_in_dim.124), calls=%async_computation.15 | async-start | bytes 73728 | tf_op jit(solution)/shard_map/all_to_all | solution.py:27
  426.4 9.4 %all-to-all-start.35 = ((bf16[4,66,256]{2,1,0:T(8,128)(2,1)}), bf16[4,66,256]{2,1,0:T(8,128)(2,1)S(1)}, u32[]{:S(2)}, u32[]{:S(2)}) async-start(bf16[4,66,256]{2,1,0:T(8,128)(2,1)} %broadcast_in_dim.137), calls=%async_computation.35 | async-start | bytes 294912 | tf_op jit(solution)/shard_map/all_to_all | solution.py:27
  436.5 9.4 %all-to-all-start.16 = ((bf16[4,66,256]{2,1,0:T(8,128)(2,1)}), bf16[4,66,256]{2,1,0:T(8,128)(2,1)S(1)}, u32[]{:S(2)}, u32[]{:S(2)}) async-start(bf16[4,66,256]{2,1,0:T(8,128)(2,1)} %broadcast_in_dim.127), calls=%async_computation.16 | async-start | bytes 294912 | tf_op jit(solution)/shard_map/all_to_all | solution.py:27
  445.9 11.5 %all-to-all-start.36 = ((bf16[4,32,128]{2,0,1:T(4,128)(2,1)}), bf16[4,32,128]{2,0,1:T(4,128)(2,1)S(1)}, u32[]{:S(2)}, u32[]{:S(2)}) async-start(bf16[4,32,128]{2,0,1:T(4,128)(2,1)} %copy.127), calls=%async_computation.36 | async-start | bytes 65536 | tf_op jit(solution)/shard_map/all_to_all | solution.py:84
  457.3 11.3 %all-to-all-start.17 = ((bf16[4,32,128]{2,0,1:T(4,128)(2,1)}), bf16[4,32,128]{2,0,1:T(4,128)(2,1)S(1)}, u32[]{:S(2)}, u32[]{:S(2)}) async-start(bf16[4,32,128]{2,0,1:T(4,128)(2,1)} %copy.107), calls=%async_computation.17 | async-start | bytes 65536 | tf_op jit(solution)/shard_map/all_to_all | solution.py:84
  468.6 15.5 %all-to-all-start.37 = ((f32[32,4,1024]{2,1,0:T(4,128)}), f32[32,4,1024]{2,1,0:T(4,128)S(1)}, u32[]{:S(2)}, u32[]{:S(2)}) async-start(f32[32,4,1024]{2,1,0:T(4,128)} %copy.129), calls=%async_computation.37 | async-start | bytes 1048576 | tf_op jit(solution)/shard_map/all_to_all | solution.py:21
  484.1 15.5 %all-to-all-start.18 = ((f32[32,4,1024]{2,1,0:T(4,128)}), f32[32,4,1024]{2,1,0:T(4,128)S(1)}, u32[]{:S(2)}, u32[]{:S(2)}) async-start(f32[32,4,1024]{2,1,0:T(4,128)} %copy.109), calls=%async_computation.18 | async-start | bytes 1048576 | tf_op jit(solution)/shard_map/all_to_all | solution.py:21
  (80 other events, 344.8 us)
where the time goes:
time: 506 us; the launch traced here: 500 us
  waiting for transfers between devices  225 us (44%)
  starting transfers between devices  118 us (23%)
  blocking collectives  83.9 us (17%)
  local copies, waits for them, and re-layouts  41.5 us (8%)
  other arithmetic  19.1 us (4%)
  matrix products  11.1 us (2%)
    all_to_all x12, waiting for transfers between devices, sent_and_summed(): lax.all_to_all(cut_along(array, dim, devices), axis, 0, 0, tiled=True)  136 us
    all_to_all x12, starting transfers between devices, sent_and_summed(): lax.all_to_all(cut_along(array, dim, devices), axis, 0, 0, tiled=True)  51.1 us
    all_to_all x8, waiting for transfers between devices, spread_project(): lax.all_to_all(normed, 'dp', split_axis=1, concat_axis=0, tiled=True)  44.9 us
    all_to_all x9, waiting for transfers between devices, from_everyone(): return lax.all_to_all(copies, axis, split_axis=0, concat_axis=0, tiled=True)  44.2 us
    all_to_all x4, blocking collectives, spread_project(): lax.all_to_all(normed, 'dp', split_axis=1, concat_axis=0, tiled=True)  43.3 us
    all_to_all x5, blocking collectives, from_everyone(): return lax.all_to_all(copies, axis, split_axis=0, concat_axis=0, tiled=True)  40.6 us
    all_to_all x8, starting transfers between devices, spread_project(): lax.all_to_all(normed, 'dp', split_axis=1, concat_axis=0, tiled=True)  34.5 us
    all_to_all x9, starting transfers between devices, from_everyone(): return lax.all_to_all(copies, axis, split_axis=0, concat_axis=0, tiled=True)  31.9 us
  transfers between devices with their start and end apart: 29, of which 29 were waited for; matrix products, arithmetic and copies ran while one was open for 8% of the time, Pallas kernels for 0%

commit v1 on v0

v1 whole, which is shorter than its diff:
```python
import jax
import jax.numpy as jnp
from jax import lax
from jax.experimental import pallas as pl
from jax.experimental.pallas import tpu as pltpu
from jax.sharding import PartitionSpec as P

HEADS = 16
HEAD_DIM = 256
WIN = 2048
LAYERS = 2
STEPS = 2
F32 = jnp.float32
BF16 = jnp.bfloat16
MESH = pl.DeviceIdType.MESH

NDP = 32
NMP = 4
ROWS = 8
SEQ = 4
FEAT = 1024
PIECE = 256
HALF = 512
SLOTS = 512
WIDTHS = (1024, 512, 1024, 512, 640, 512)


def kernel(
    hidden_in,
    rec_gain,
    rec_in_x,
    rec_in_y,
    conv_weight,
    conv_bias,
    gate_x_weight,
    gate_x_bias,
    gate_a_weight,
    gate_a_bias,
    decay_param,
    rec_out,
    lru_state,
    conv_state,
    scale_index,
    attn_gain,
    attn_q,
    attn_kv,
    attn_out,
    key_cache,
    value_cache,
    positions,
    hidden_out,
    lru_out,
    conv_out,
    new_kv,
    hid_v,
    rgain_v,
    again_v,
    cw_v,
    cb_v,
    gxw_v,
    gxb_v,
    gaw_v,
    gab_v,
    dec_v,
    lru_v,
    conv_v,
    key_v,
    val_v,
    wkv_v,
    win0,
    win1,
    wout0,
    wout1,
    wq,
    wo,
    scale_s,
    pos_s,
    x_v,
    f8,
    st_v,
    t0_v,
    t1_v,
    t2_v,
    mask_v,
    asend,
    abuf,
    bs0,
    bs1,
    bs2,
    bs3,
    bs4,
    bs5,
    bb0,
    bb1,
    bb2,
    bb3,
    bb4,
    bb5,
    nsend,
    nbuf,
    zsend,
    zbuf,
    csend,
    cbuf,
    tsend,
    tbuf,
    lsem,
    wsend,
    wrecv,
    asnd,
    arcv,
    bsnd,
    brcv,
    nsnd,
    nrcv,
    zsnd,
    zrcv,
    csnd,
    crcv,
    tsnd,
    trcv,
):
    i = lax.axis_index("dp")
    j = lax.axis_index("mp")
    core = lax.rem(i, 2)
    mate = i + 1 - 2 * core
    yy = lax.div(i, 8)
    xx = lax.div(lax.rem(i, 8), 2)
    bsend = (bs0, bs1, bs2, bs3, bs4, bs5)
    bbuf = (bb0, bb1, bb2, bb3, bb4, bb5)

    def local(src, dst, k):
        copy = pltpu.make_async_copy(src, dst, lsem.at[k])
        copy.start()
        return copy

    fcol = pl.ds(pl.multiple_of(j * FEAT, FEAT), FEAT)
    mine = pl.ds(pl.multiple_of(core * HALF, HALF), HALF)
    other = pl.ds(pl.multiple_of((1 - core) * HALF, HALF), HALF)
    krow = pl.ds(pl.multiple_of(core * 128, 128), 128)

    c_hid = local(hidden_in, hid_v, 0)
    c_rg = local(rec_gain.at[:, fcol], rgain_v, 1)

    barrier = pltpu.get_barrier_semaphore()

    def greet_plane(k, _):
        @pl.when(jnp.logical_not((k == i) & (yy == j)))
        def _():
            pl.semaphore_signal(barrier, inc=1, device_id=(k, yy), device_id_type=MESH)

        return 0

    lax.fori_loop(0, NDP, greet_plane, 0)

    def greet_dp(k, _):
        pl.semaphore_signal(
            barrier, inc=1, device_id=(lax.rem(i + k, NDP), j), device_id_type=MESH
        )
        return 0

    lax.fori_loop(1, NDP, greet_dp, 0)

    def greet_mp(k, _):
        pl.semaphore_signal(
            barrier, inc=1, device_id=(i, lax.rem(j + k, NMP)), device_id_type=MESH
        )
        return 0

    lax.fori_loop(1, NMP, greet_mp, 0)

    weights = (
        (rec_in_x.at[0], win0, 0),
        (rec_in_y.at[0], win0, HALF),
        (rec_out.at[0], wout0, 0),
        (rec_in_x.at[1], win1, 0),
        (rec_in_y.at[1], win1, HALF),
        (rec_out.at[1], wout1, 0),
        (attn_q, wq, 0),
        (attn_out, wo, 0),
    )
    c_w = [
        local(src.at[:, mine], dst.at[krow, pl.ds(at, HALF)], 2 + k)
        for k, (src, dst, at) in enumerate(weights)
    ]
    c_lru = local(lru_state, lru_v, 10)
    c_conv = local(conv_state, conv_v, 11)
    c_sc = local(scale_index, scale_s, 12)
    c_pos = local(positions, pos_s, 13)
    c_cw = local(conv_weight, cw_v, 14)
    c_cb = local(conv_bias, cb_v, 15)
    c_gxb = local(gate_x_bias, gxb_v, 16)
    c_gab = local(gate_a_bias, gab_v, 17)
    c_dec = local(decay_param, dec_v, 18)
    c_gxw = local(gate_x_weight, gxw_v, 19)
    c_gaw = local(gate_a_weight, gaw_v, 20)
    c_ag = local(attn_gain.at[:, fcol], again_v, 21)
    c_wkv = local(attn_kv, wkv_v, 22)
    c_key = local(key_cache, key_v, 23)
    c_val = local(value_cache, val_v, 24)

    row = lax.broadcasted_iota(jnp.int32, (ROWS, FEAT), 0)
    late = row >= SEQ

    def norm_send(k):
        x = x_v[...]
        sq = jnp.sum(x * x, axis=-1, keepdims=True)
        sq = jnp.broadcast_to(sq, (ROWS, 128))
        nsend[k] = sq
        nbuf[k, j] = sq

        def one(d, _):
            pltpu.make_async_remote_copy(
                src_ref=nsend.at[k],
                dst_ref=nbuf.at[k, j],
                send_sem=nsnd.at[k],
                recv_sem=nrcv.at[k],
                device_id=(i, lax.rem(j + d, NMP)),
                device_id_type=MESH,
            ).start()
            return 0

        lax.fori_loop(1, NMP, one, 0)

    def norm_scale(k):
        view = nbuf.at[k, pl.ds(0, NMP - 1)]
        pltpu.make_async_copy(view, view, nrcv.at[k]).wait()
        total = (nbuf[k, 0] + nbuf[k, 1]) + (nbuf[k, 2] + nbuf[k, 3])
        return lax.rsqrt(total[:, :1] * (1.0 / 4096.0) + 1e-06)

    def spread(k):
        def one(n, _):
            q = lax.div(n, NMP)
            z = lax.rem(n, NMP)
            d = 8 * j + q

            @pl.when(jnp.logical_not((d == i) & (z == j)))
            def _():
                pltpu.make_async_remote_copy(
                    src_ref=asend.at[k, lax.div(q, 2)],
                    dst_ref=abuf.at[k, i],
                    send_sem=asnd.at[k],
                    recv_sem=arcv.at[k],
                    device_id=(d, z),
                    device_id_type=MESH,
                ).start()

            return 0

        lax.fori_loop(0, NDP, one, 0)

        @pl.when(yy == j)
        def _():
            abuf[k, i] = asend[k, xx]

    def spread_wait(k):
        @pl.when(yy == j)
        def _():
            view = abuf.at[k, pl.ds(0, NDP - 1)]
            pltpu.make_async_copy(view, view, arcv.at[k]).wait()

        @pl.when(yy != j)
        def _():
            view = abuf.at[k]
            pltpu.make_async_copy(view, view, arcv.at[k]).wait()

    def arrived(k):
        spread_wait(k)
        return abuf[k].astype(F32).reshape(NDP * ROWS, PIECE).astype(BF16)

    def project(k, act, weight, width):
        for n in range(width // PIECE):
            cols = slice(n * PIECE, (n + 1) * PIECE)
            part = jnp.dot(act, weight[:, cols], preferred_element_type=F32)
            bsend[k][:, :, cols] = part.reshape(NDP, ROWS, PIECE).astype(BF16)

    def reduce_send(k):
        def one(n, _):
            d = lax.rem(i + n, NDP)
            pltpu.make_async_remote_copy(
                src_ref=bsend[k].at[d],
                dst_ref=bbuf[k].at[i],
                send_sem=bsnd.at[k],
                recv_sem=brcv.at[k],
                device_id=(d, j),
                device_id_type=MESH,
            ).start()
            return 0

        lax.fori_loop(1, NDP, one, 0)
        bbuf[k][i] = bsend[k][i]

    def reduce_wait(k):
        view = bbuf[k].at[pl.ds(0, NDP - 1)]
        pltpu.make_async_copy(view, view, brcv.at[k]).wait()

    def summed(k, c, cols):
        acc = bbuf[k][c, :, cols].astype(F32)
        for p in range(1, NDP // 2):
            acc = acc + bbuf[k][2 * p + c, :, cols].astype(F32)
        return acc

    def set_pieces(k, values):
        for q in range(NMP):
            asend[k, q] = values[:, q * PIECE : (q + 1) * PIECE].astype(BF16)

    c_hid.wait()
    c_rg.wait()
    x_v[0:SEQ, :] = hid_v[0].astype(F32)
    x_v[SEQ:ROWS, :] = hid_v[1].astype(F32)
    set_pieces(0, x_v[...] * rgain_v[0:1, :])

    met = 2 * NDP - 1 + NMP - 1
    pl.semaphore_wait(barrier, jnp.where(yy == j, met - 1, met))

    spread(0)
    w_out = [
        pltpu.make_async_remote_copy(
            src_ref=src.at[:, other],
            dst_ref=dst.at[krow, pl.ds(at, HALF)],
            send_sem=wsend.at[k],
            recv_sem=wrecv.at[k],
            device_id=(mate, j),
            device_id_type=MESH,
        )
        for k, (src, dst, at) in enumerate(weights)
    ]
    for copy in w_out:
        copy.start()
    norm_send(0)

    c_lru.wait()
    c_conv.wait()
    c_sc.wait()
    scales = []
    for l in range(LAYERS):
        power = (scale_s[l].astype(F32) - 4.0) * 0.5
        scales.append(jnp.exp2(jnp.full((1, 128), power, F32))[:, :1])
        st_v[l, 0:SEQ, :] = lru_v[l].astype(F32) * scales[l]
        st_v[l, SEQ:ROWS, :] = jnp.zeros((SEQ, FEAT), F32)
        w0 = conv_v[l, 0].astype(F32)
        w1 = conv_v[l, 1].astype(F32)
        w2 = conv_v[l, 2].astype(F32)
        t0_v[l, 0:SEQ, :] = w0
        t0_v[l, SEQ:ROWS, :] = w1
        t1_v[l, 0:SEQ, :] = w1
        t1_v[l, SEQ:ROWS, :] = w2
        t2_v[l, 0:SEQ, :] = w2
        t2_v[l, SEQ:ROWS, :] = jnp.zeros((SEQ, FEAT), F32)
        conv_out[l, 0] = conv_v[l, 2]
    c_pos.wait()
    srow = lax.broadcasted_iota(jnp.int32, (ROWS, SLOTS), 0)
    slot = lax.broadcasted_iota(jnp.int32, (ROWS, SLOTS), 1) + j * SLOTS
    seq = srow & 3
    pos = jnp.where(
        seq == 0, pos_s[0], jnp.where(seq == 1, pos_s[1], jnp.where(seq == 2, pos_s[2], pos_s[3]))
    )
    step = lax.shift_right_logical(srow, 2)
    held = pos - 1 - ((pos - 1 - slot) & (WIN - 1))
    mask_v[...] = jnp.where((held >= 0) & (held >= pos + step - (WIN - 1)), 1.0, 0.0).astype(F32)
    for copy in (c_cw, c_cb, c_gxb, c_gab, c_dec, c_gxw, c_gaw):
        copy.wait()

    def recurrent(l):
        ka, kb = 2 * l, 2 * l + 1
        weight = (win0, win1)[l]
        for k in (3 * l, 3 * l + 1):
            c_w[k].wait()
            w_out[k].wait_recv()
        act = arrived(ka)
        project(ka, act, weight, 2 * HALF)
        reduce_send(ka)
        scale = norm_scale(l)
        decay = dec_v[l : l + 1, :]
        soft = jnp.maximum(decay, 0.0) + jnp.log1p(jnp.exp(-jnp.abs(decay)))
        partial_taps = (
            cw_v[l, 0:1, :] * t0_v[l] + cw_v[l, 1:2, :] * t1_v[l] + cb_v[l : l + 1, :]
        )
        reduce_wait(ka)
        for c in range(2):
            cols = slice(c * HALF, (c + 1) * HALF)
            u = summed(ka, c, slice(0, HALF)) * scale
            f8[0, :, cols] = u.astype(BF16).astype(F32)
            f8[1, :, cols] = summed(ka, c, slice(HALF, 2 * HALF)) * scale
        u = f8[0]
        v = f8[1]
        u_roll = pltpu.roll(u, SEQ, 0)
        conv_out[l, 1] = u[0:SEQ].astype(BF16)
        conv_out[l, 2] = u_roll[0:SEQ].astype(BF16)
        t2 = jnp.where(late, u_roll, t2_v[l])
        filtered = partial_taps + cw_v[l, 2:3, :] * t2 + cw_v[l, 3:4, :] * u
        half = filtered.astype(BF16)
        for b in range(4):
            cols = slice(b * PIECE, (b + 1) * PIECE)
            f8[2, :, cols] = jnp.dot(half[:, cols], gxw_v[l, b], preferred_element_type=F32)
            f8[3, :, cols] = jnp.dot(half[:, cols], gaw_v[l, b], preferred_element_type=F32)
        gi = 1.0 / (1.0 + jnp.exp(-(f8[2] + gxb_v[l : l + 1, :])))
        ga = 1.0 / (1.0 + jnp.exp(-(f8[3] + gab_v[l : l + 1, :])))
        log_a = -8.0 * ga * soft
        a = jnp.exp(log_a)
        add = jnp.sqrt(1.0 - jnp.exp(2.0 * log_a)) * (gi * filtered)
        first = a * st_v[l] + add
        second = a * pltpu.roll(first, SEQ, 0) + add
        state = jnp.where(late, second, first)
        gelu = 0.5 * v * (1.0 + jnp.tanh(0.7978845608028654 * (v + 0.044715 * (v * v * v))))
        set_pieces(kb, state * gelu)
        spread(kb)
        lru_out[l] = (pltpu.roll(state, SEQ, 0)[0:SEQ] / scales[l]).astype(BF16)

        k = 3 * l + 2
        c_w[k].wait()
        w_out[k].wait_recv()
        act = arrived(kb)
        project(kb, act, (wout0, wout1)[l], HALF)
        reduce_send(kb)
        reduce_wait(kb)
        for c in range(2):
            cols = slice(c * HALF, (c + 1) * HALF)
            x_v[:, cols] = x_v[:, cols] + summed(kb, c, slice(0, HALF))

    recurrent(0)
    set_pieces(2, x_v[...] * rgain_v[1:2, :])
    spread(2)
    norm_send(1)
    recurrent(1)
    c_ag.wait()
    set_pieces(4, x_v[...] * again_v[...])
    spread(4)
    norm_send(2)

    for copy in (c_wkv, c_key, c_val, c_w[6], c_w[7]):
        copy.wait()
    w_out[6].wait_recv()
    act = arrived(4)
    project(4, act, wq, HALF)
    own = pl.ds(pl.multiple_of(core * 128, 128), 128)
    act = abuf[4, :, :, own].astype(F32).reshape(NDP * ROWS, 128).astype(BF16)
    part = jnp.dot(act, wkv_v[...], preferred_element_type=F32)
    bs4[:, :, HALF:] = part.reshape(NDP, ROWS, 128).astype(BF16)
    reduce_send(4)
    scale = norm_scale(2)
    reduce_wait(4)
    for c in range(2):
        zsend[:, c * HALF : (c + 1) * HALF] = (summed(4, c, slice(0, HALF)) * scale).astype(BF16)
    kv = (summed(4, 0, slice(HALF, HALF + 128)) + summed(4, 1, slice(HALF, HALF + 128))) * scale
    zsend[:, FEAT:] = kv.astype(BF16)

    def query_send(d, _):
        pltpu.make_async_remote_copy(
            src_ref=zsend,
            dst_ref=zbuf.at[j],
            send_sem=zsnd,
            recv_sem=zrcv,
            device_id=(i, lax.rem(j + d, NMP)),
            device_id_type=MESH,
        ).start()
        return 0

    lax.fori_loop(1, NMP, query_send, 0)
    zbuf[j] = zsend[...]
    new_kv[0] = kv[0:SEQ].astype(BF16)
    new_kv[1] = pltpu.roll(kv, SEQ, 0)[0:SEQ].astype(BF16)
    view = zbuf.at[pl.ds(0, NMP - 1)]
    pltpu.make_async_copy(view, view, zrcv).wait()

    rows = HEADS * ROWS
    query = jnp.concatenate(
        [
            zbuf[z, :, h * HEAD_DIM : (h + 1) * HEAD_DIM].astype(F32)
            for z in range(NMP)
            for h in range(HEADS // NMP)
        ],
        axis=0,
    ).astype(BF16)
    which = lax.broadcasted_iota(jnp.int32, (rows, SLOTS), 0) & 3
    scores = None
    for b in range(SEQ):
        one = lax.dot_general(
            query, key_v[b], (((1,), (1,)), ((), ())), preferred_element_type=F32
        )
        scores = one if scores is None else jnp.where(which == b, one, scores)
    mask = jnp.broadcast_to(mask_v[...][None], (HEADS, ROWS, SLOTS)).reshape(rows, SLOTS)
    scores = jnp.where(mask > 0.5, scores * HEAD_DIM ** (-0.5), -1e30)
    top = jnp.max(scores, axis=-1, keepdims=True)
    weight = jnp.exp(scores - top) * mask
    total = jnp.sum(weight, axis=-1, keepdims=True)
    values = None
    for b in range(SEQ):
        one = jnp.dot(
            jnp.where(which == b, weight, 0.0).astype(BF16), val_v[b], preferred_element_type=F32
        )
        values = one if values is None else values + one
    lane = lax.broadcasted_iota(jnp.int32, (rows, 128), 1)
    csend[...] = values.reshape(HEADS, ROWS, HEAD_DIM).astype(BF16)
    tsend[...] = jnp.where(lane < 64, top, total).reshape(HEADS, ROWS, 128)

    def part_send(d, _):
        z = lax.rem(j + d, NMP)
        group = pl.ds(4 * z, 4)
        pltpu.make_async_remote_copy(
            src_ref=csend.at[group],
            dst_ref=cbuf.at[j],
            send_sem=csnd,
            recv_sem=crcv,
            device_id=(i, z),
            device_id_type=MESH,
        ).start()
        pltpu.make_async_remote_copy(
            src_ref=tsend.at[group],
            dst_ref=tbuf.at[j],
            send_sem=tsnd,
            recv_sem=trcv,
            device_id=(i, z),
            device_id_type=MESH,
        ).start()
        return 0

    lax.fori_loop(1, NMP, part_send, 0)
    cbuf[j] = csend[pl.ds(4 * j, 4)]
    tbuf[j] = tsend[pl.ds(4 * j, 4)]

    lateh = lax.broadcasted_iota(jnp.int32, (ROWS, HEAD_DIM), 0) >= SEQ
    late1 = lax.broadcasted_iota(jnp.int32, (ROWS, 1), 0) >= SEQ

    def pair(lo, hi):
        at = slice(FEAT, FEAT + 128)
        both = jnp.concatenate([zbuf[lo, :, at].astype(F32), zbuf[hi, :, at].astype(F32)], axis=1)
        turned = pltpu.roll(both, SEQ, 0)
        return jnp.where(lateh, turned, both), jnp.where(lateh, both, turned)

    key0, key1 = pair(0, 1)
    val0, val1 = pair(2, 3)
    fresh = []
    for h in range(4):
        head = zsend[:, h * HEAD_DIM : (h + 1) * HEAD_DIM].astype(F32)
        s0 = jnp.sum(head * key0, axis=-1, keepdims=True) * HEAD_DIM ** (-0.5)
        s1 = jnp.sum(head * key1, axis=-1, keepdims=True) * HEAD_DIM ** (-0.5)
        fresh.append((s0, jnp.where(late1, s1, -1e30)))
    view = cbuf.at[pl.ds(0, NMP - 1)]
    pltpu.make_async_copy(view, view, crcv).wait()
    view = tbuf.at[pl.ds(0, NMP - 1)]
    pltpu.make_async_copy(view, view, trcv).wait()
    for h in range(4):
        s0, s1 = fresh[h]
        tops = [tbuf[z, h, :, 0:1] for z in range(NMP)]
        best = jnp.maximum(s0, s1)
        for t in tops:
            best = jnp.maximum(best, t)
        w0 = jnp.exp(s0 - best)
        w1 = jnp.where(late1, jnp.exp(s1 - best), 0.0)
        den = w0 + w1
        num = w0.astype(BF16).astype(F32) * val0 + w1.astype(BF16).astype(F32) * val1
        for z in range(NMP):
            fade = jnp.exp(tops[z] - best)
            den = den + fade * tbuf[z, h, :, 64:65]
            num = num + fade * cbuf[z, h].astype(F32)
        asend[5, h] = (num / den).astype(BF16)
    spread(5)
    w_out[7].wait_recv()
    act = arrived(5)
    project(5, act, wo, HALF)
    reduce_send(5)
    reduce_wait(5)
    for c in range(2):
        cols = slice(c * HALF, (c + 1) * HALF)
        x_v[:, cols] = x_v[:, cols] + summed(5, c, slice(0, HALF))
    x = x_v[...]
    hidden_out[0] = x[0:SEQ].astype(BF16)
    hidden_out[1] = pltpu.roll(x, SEQ, 0)[0:SEQ].astype(BF16)

    for copy in w_out:
        copy.wait_send()
    for k in range(3):
        view = nbuf.at[k, pl.ds(0, NMP - 1)]
        pltpu.make_async_copy(view, view, nsnd.at[k]).wait()
    for k in range(6):
        view = bbuf[k].at[pl.ds(0, NDP - 1)]
        pltpu.make_async_copy(view, view, bsnd.at[k]).wait()

        @pl.when(yy == j)
        def _():
            view = abuf.at[k, pl.ds(0, NDP - 1)]
            pltpu.make_async_copy(view, view, asnd.at[k]).wait()

        @pl.when(yy != j)
        def _():
            view = abuf.at[k]
            pltpu.make_async_copy(view, view, asnd.at[k]).wait()

    for buf, sem in ((zbuf, zsnd), (cbuf, csnd), (tbuf, tsnd)):
        view = buf.at[pl.ds(0, NMP - 1)]
        pltpu.make_async_copy(view, view, sem).wait()


def body(*args):
    args = list(args)
    args[15] = args[15].reshape(1, -1)
    shape = jax.ShapeDtypeStruct
    hbm = pl.BlockSpec(memory_space=pl.ANY)
    vmem = pl.BlockSpec(memory_space=pltpu.VMEM)
    V = pltpu.VMEM
    DMA = pltpu.SemaphoreType.DMA
    scratch = [
        V((STEPS, SEQ, FEAT), BF16),
        V((LAYERS, FEAT), F32),
        V((1, FEAT), F32),
        V((LAYERS, 4, FEAT), F32),
        V((LAYERS, FEAT), F32),
        V((LAYERS, 4, PIECE, PIECE), BF16),
        V((LAYERS, FEAT), F32),
        V((LAYERS, 4, PIECE, PIECE), BF16),
        V((LAYERS, FEAT), F32),
        V((LAYERS, FEAT), F32),
        V((LAYERS, SEQ, FEAT), BF16),
        V((LAYERS, 3, SEQ, FEAT), BF16),
        V((SEQ, SLOTS, HEAD_DIM), BF16),
        V((SEQ, SLOTS, HEAD_DIM), BF16),
        V((128, 128), BF16),
        V((PIECE, 2 * HALF), BF16),
        V((PIECE, 2 * HALF), BF16),
        V((PIECE, HALF), BF16),
        V((PIECE, HALF), BF16),
        V((PIECE, HALF), BF16),
        V((PIECE, HALF), BF16),
        pltpu.SMEM((LAYERS,), jnp.int32),
        pltpu.SMEM((SEQ,), jnp.int32),
        V((ROWS, FEAT), F32),
        V((4, ROWS, FEAT), F32),
        V((LAYERS, ROWS, FEAT), F32),
        V((LAYERS, ROWS, FEAT), F32),
        V((LAYERS, ROWS, FEAT), F32),
        V((LAYERS, ROWS, FEAT), F32),
        V((ROWS, SLOTS), F32),
        V((6, NMP, ROWS, PIECE), BF16),
        V((6, NDP, ROWS, PIECE), BF16),
        *[V((NDP, ROWS, w), BF16) for w in WIDTHS],
        *[V((NDP, ROWS, w), BF16) for w in WIDTHS],
        V((3, ROWS, 128), F32),
        V((3, NMP, ROWS, 128), F32),
        V((ROWS, FEAT + 128), BF16),
        V((NMP, ROWS, FEAT + 128), BF16),
        V((HEADS, ROWS, HEAD_DIM), BF16),
        V((NMP, 4, ROWS, HEAD_DIM), BF16),
        V((HEADS, ROWS, 128), F32),
        V((NMP, 4, ROWS, 128), F32),
        DMA((25,)),
        DMA((8,)),
        DMA((8,)),
        DMA((6,)),
        DMA((6,)),
        DMA((6,)),
        DMA((6,)),
        DMA((3,)),
        DMA((3,)),
        DMA,
        DMA,
        DMA,
        DMA,
        DMA,
        DMA,
    ]
    return pl.pallas_call(
        kernel,
        out_shape=(
            shape((STEPS, SEQ, FEAT), BF16),
            shape((LAYERS, SEQ, FEAT), BF16),
            shape((LAYERS, 3, SEQ, FEAT), BF16),
            shape((STEPS, SEQ, 128), BF16),
        ),
        in_specs=[hbm] * 22,
        out_specs=(vmem,) * 4,
        scratch_shapes=scratch,
        compiler_params=pltpu.CompilerParams(
            collective_id=0, has_side_effects=True, vmem_limit_bytes=40 * 1024 * 1024
        ),
    )(*args)


def solution(mesh):
    placed = (
        P(None, "dp", "mp"),
        P(),
        P(None, "dp", "mp"),
        P(None, "dp", "mp"),
        P(None, None, "mp"),
        P(None, "mp"),
        P(None, "mp", None, None),
        P(None, "mp"),
        P(None, "mp", None, None),
        P(None, "mp"),
        P(None, "mp"),
        P(None, "dp", "mp"),
        P(None, "dp", "mp"),
        P(None, None, "dp", "mp"),
        P(),
        P(),
        P("dp", "mp"),
        P("dp", "mp"),
        P("dp", "mp"),
        P("dp", "mp", None),
        P("dp", "mp", None),
        P("dp"),
    )
    return jax.shard_map(
        body,
        mesh=mesh,
        in_specs=placed,
        out_specs=(
            P(None, "dp", "mp"),
            P(None, "dp", "mp"),
            P(None, None, "dp", "mp"),
            P(None, "dp", "mp"),
        ),
        check_vma=False,
    )
```

time: 506 us -> 137 us (0.27)
  waiting for transfers between devices: 225 us -> 0 us
  starting transfers between devices: 118 us -> 0 us
  Pallas kernels: 0 us -> 113 us
  blocking collectives: 83.9 us -> 0 us
  local copies, waits for them, and re-layouts: 41.5 us -> 21 us
  other arithmetic: 19.1 us -> 0 us
  matrix products: 11.1 us -> 0 us
    all_to_all x29 -> x0, waiting for transfers between devices: 225 us -> none  [the longest x12 136 us: sent_and_summed(): lax.all_to_all(cut_along(array, dim, devices), axis, 0, 0, tiled=True)]
    all_to_all x29 -> x0, starting transfers between devices: 118 us -> none  [the longest x12 51.1 us: sent_and_summed(): lax.all_to_all(cut_along(array, dim, devices), axis, 0, 0, tiled=True)]
    pallas_call x0 -> x1, Pallas kernels: none -> 113 us  [body(): pl.pallas_call(kernel, out_shape=(shape((STEPS, SEQ, FEAT), BF16), shape(...]
    all_to_all x9 -> x0, blocking collectives: 83.9 us -> none  [the longest x4 43.3 us: spread_project(): lax.all_to_all(normed, 'dp', split_axis=1, concat_axis=0, tiled=True)]
    dot_general x12 -> x0, local copies, waits for them, and re-layouts: 15.9 us -> none  [spread_project(): jnp.dot(spread, weight, preferred_element_type=jnp.float32)]
    dot_general x27 -> x0, matrix products: 11.1 us -> none  [the longest x12 7.68 us: spread_project(): jnp.dot(spread, weight, preferred_element_type=jnp.float32)]
    unnamed x170 -> x48, local copies, waits for them, and re-layouts: 10 us -> 21 us
    reduce_sum x23 -> x0, other arithmetic: 8.62 us -> none  [the longest x12 7.23 us: sent_and_summed(): return jnp.sum(pieces, axis=0)]
  transfers between devices with their start and end apart: 29 -> 0, of which waited for: 29 -> 0; matrix products, arithmetic and copies ran while one was open for 8% -> 0% of each run, Pallas kernels for 0% -> 0%
where the time goes in v1:
time: 137 us; the launch traced here: 134 us
  Pallas kernels  113 us (82%)
  local copies, waits for them, and re-layouts  21 us (15%)
    pallas_call x1, Pallas kernels, body(): pl.pallas_call(kernel, out_shape=(shape((STEPS, SEQ, FEAT), BF16), shape(...  113 us
    unnamed x48, local copies, waits for them, and re-layouts  21 us

profile of v1, /device:TPU:0, one launch (start us, length us, event | category | flops | bytes accessed | tf_op | source)
XLA Modules:
  0.0 134.4 jit_solution(17348757365783498135)
XLA Ops:
  0.6 0.0 copy-start.21
  0.7 0.0 copy-start.20
  0.7 0.6 copy-done.21
  1.3 0.0 copy-done.20
  1.3 0.0 copy-start
  1.3 1.2 copy-done
  2.5 1.2 copy-done.1
  3.8 0.0 copy-start.2
  3.8 1.2 copy-done.2
  5.0 0.0 copy-start.3
  5.0 1.2 copy-done.3
  6.2 1.0 copy-done.4
  7.3 1.0 copy-done.5
  8.3 1.0 copy-done.6
  9.3 0.9 copy-done.7
  10.3 0.9 copy-done.8
  11.2 0.8 copy-done.9
  12.0 0.8 copy-done.10
  12.8 0.8 copy-done.11
  13.6 0.8 copy-done.12
  14.3 0.7 copy-done.13
  15.0 0.7 copy-done.14
  15.8 0.7 copy-done.15
  16.5 0.7 copy-done.16
  17.2 0.7 copy-done.17
  17.9 0.7 copy-done.18
  18.6 0.7 copy-done.19
  19.3 112.8 %shard_map.237 = (bf16[2,4,1024]{2,1,0:T(4,128)(2,1)S(1)}, bf16[2,4,1024]{2,1,0:T(4,128)(2,1)S(1)}, bf16[2,3,4,1024]{3,2,1,0:T(4,128)(2,1)S(1)}, bf16[2,4,128]{2,1,0:T(4,128)(2,1)S(1)}) custom-call(bf16[2,4,1024]{2,1,0:T(4,128)(2,1)S(1)} %copy-done.13, f32[2,4096]{1,0:T(2,128)S(1)} %copy-done.10, bf16[2,128,1024]{2,1,0:T(8,128)(2,1)S(1)} %copy-done.4, ...), custom_call_target="tpu_custom_call" | custom-call | tf_op jit(solution)/shard_map/pallas_call | solution.py:662
  132.0 0.6 copy.30
  132.6 0.6 copy.31
  133.2 0.6 copy.32
  133.9 0.6 copy.33
  (17 shorter events, 0.0 us)
Async XLA Ops:
  0.6 0.7 copy-start.21
  0.7 0.7 copy-start.20
  1.3 1.2 copy-start
  2.5 1.2 copy-start.1
  3.8 1.2 copy-start.2
  5.0 1.2 copy-start.3
  6.2 1.0 copy-start.4
  7.3 1.0 copy-start.5
  8.3 1.0 copy-start.6
  9.3 0.9 copy-start.7
  10.3 0.9 copy-start.8
  11.2 0.8 copy-start.9
  12.0 0.8 copy-start.10
  12.8 0.8 copy-start.11
  13.6 0.8 copy-start.12
  14.3 0.7 copy-start.13
  15.0 0.7 copy-start.14
  15.8 0.7 copy-start.15
  16.5 0.7 copy-start.16
  17.2 0.7 copy-start.17
  17.9 0.7 copy-start.18
  18.6 0.7 copy-start.19

commit v2 on v0

v2 whole, which is shorter than its diff:
```python
import jax
import jax.numpy as jnp
from jax import lax
from jax.experimental import pallas as pl
from jax.experimental.pallas import tpu as pltpu
from jax.sharding import PartitionSpec as P

HEADS = 16
HEAD_DIM = 256
WIN = 2048
LAYERS = 2
STEPS = 2
F32 = jnp.float32
BF16 = jnp.bfloat16
MESH = pl.DeviceIdType.MESH

NDP = 32
NMP = 4
NX = 4
ROWS = 8
SEQ = 4
FEAT = 1024
PIECE = 256
HALF = 512
SLOTS = 512
BLOCKS = 8
BLOCK = 32
CHIPS = 16
VMEM = 67043328


def scratch_list():
    V = pltpu.VMEM
    DMA = pltpu.SemaphoreType.DMA
    return [
        ("hid_v", V((STEPS, SEQ, FEAT), BF16)),
        ("rgain_v", V((2, LAYERS, PIECE), F32)),
        ("again_v", V((1, PIECE), F32)),
        ("cw_v", V((LAYERS, 4, PIECE), F32)),
        ("cb_v", V((LAYERS, PIECE), F32)),
        ("gxw_v", V((LAYERS, PIECE, PIECE), BF16)),
        ("gxb_v", V((LAYERS, PIECE), F32)),
        ("gaw_v", V((LAYERS, PIECE, PIECE), BF16)),
        ("gab_v", V((LAYERS, PIECE), F32)),
        ("dec_v", V((LAYERS, PIECE), F32)),
        ("win_v", V((LAYERS, 3, SEQ, FEAT), BF16)),
        ("key_v", V((SEQ, SLOTS, HEAD_DIM), BF16)),
        ("val_v", V((SEQ, SLOTS, HEAD_DIM), BF16)),
        ("wkv_v", V((128, 128), BF16)),
        ("wi", V((LAYERS, PIECE, 2 * HALF), BF16)),
        ("wr", V((LAYERS, PIECE, HALF), BF16)),
        ("wq", V((PIECE, HALF), BF16)),
        ("wo", V((PIECE, HALF), BF16)),
        ("scale_s", pltpu.SMEM((LAYERS,), jnp.int32)),
        ("pos_s", pltpu.SMEM((SEQ,), jnp.int32)),
        ("x_v", V((NX, ROWS, PIECE), F32)),
        ("h_v", V((ROWS, FEAT), F32)),
        ("st_v", V((LAYERS, NX, ROWS, PIECE), F32)),
        ("t0_v", V((LAYERS, NX, ROWS, PIECE), F32)),
        ("t1_v", V((LAYERS, NX, ROWS, PIECE), F32)),
        ("t2_v", V((LAYERS, NX, ROWS, PIECE), F32)),
        ("mask_v", V((ROWS, SLOTS), F32)),
        ("lru_b", V((NX, LAYERS, SEQ, PIECE), BF16)),
        ("win_b", V((NX, LAYERS, 3, SEQ, PIECE), BF16)),
        ("lru_s", V((LAYERS, NX, SEQ, PIECE), BF16)),
        ("win_s", V((LAYERS, NX, 2, SEQ, PIECE), BF16)),
        ("pieces", V((2, NMP, ROWS, PIECE), BF16)),
        ("spread_b", V((2, 2, CHIPS, ROWS, PIECE), BF16)),
        ("act_s", V((4, BLOCK, PIECE), BF16)),
        ("act_b", V((4, 2, 4, BLOCK, PIECE), BF16)),
        ("in_s", V((LAYERS, 2, BLOCKS, BLOCK, HALF), BF16)),
        ("in_b", V((LAYERS, CHIPS, BLOCK, HALF), BF16)),
        ("out_s", V((LAYERS, 2, BLOCKS, BLOCK, PIECE), BF16)),
        ("out_b", V((LAYERS, CHIPS, BLOCK, PIECE), BF16)),
        ("q_s", V((NDP, ROWS, HALF + 128), BF16)),
        ("q_b", V((NDP, ROWS, HALF + 128), BF16)),
        ("o_s", V((NDP, ROWS, HALF), BF16)),
        ("o_b", V((NDP, ROWS, HALF), BF16)),
        ("ent_b", V((NX, ROWS, PIECE), BF16)),
        ("res_s", V((NX, ROWS, PIECE), F32)),
        ("res_b", V((NX, ROWS, PIECE), F32)),
        ("nsend", V((3, 1, 128), F32)),
        ("nbuf", V((3, CHIPS, 1, 128), F32)),
        ("zsend", V((ROWS, FEAT + 128), BF16)),
        ("zbuf", V((NMP, ROWS, FEAT + 128), BF16)),
        ("csend", V((HEADS, ROWS, HEAD_DIM), BF16)),
        ("cbuf", V((NMP, 4, ROWS, HEAD_DIM), BF16)),
        ("tsend", V((HEADS, ROWS, 128), F32)),
        ("tbuf", V((NMP, 4, ROWS, 128), F32)),
        ("lsem", DMA((32,))),
        ("snd", DMA((48,))),
        ("rcv", DMA((48,))),
    ]


NAMES = (
    "hidden_in",
    "rec_gain",
    "rec_in_x",
    "rec_in_y",
    "conv_weight",
    "conv_bias",
    "gate_x_weight",
    "gate_x_bias",
    "gate_a_weight",
    "gate_a_bias",
    "decay_param",
    "rec_out",
    "lru_state",
    "conv_state",
    "scale_index",
    "attn_gain",
    "attn_q",
    "attn_kv",
    "attn_out",
    "key_cache",
    "value_cache",
    "positions",
    "hidden_out",
    "lru_out",
    "conv_out",
    "new_kv",
)


class Refs:
    def __init__(self, refs):
        names = (*NAMES, *(name for name, _ in scratch_list()))
        for name, ref in zip(names, refs, strict=True):
            setattr(self, name, ref)


def kernel(*refs):
    r = Refs(refs)
    i = lax.axis_index("dp")
    j = lax.axis_index("mp")
    core = lax.rem(i, 2)
    mate = i + 1 - 2 * core
    yy = lax.div(i, 8)
    xx = lax.div(lax.rem(i, 8), 2)
    diagonal = yy == j
    inside = lax.div(xx, 2) == core

    pending = {}
    used = [0, 0]

    def take(*names):
        for name in names:
            pending.pop(name)()

    def sems():
        used[1] += 1
        assert used[1] <= 48
        return r.snd.at[used[1] - 1], r.rcv.at[used[1] - 1]

    def local(name, src, dst):
        sem = r.lsem.at[used[0]]
        used[0] += 1
        copy = pltpu.make_async_copy(src, dst, sem)
        copy.start()
        pending[name] = copy.wait

    def remote(src, dst, pair, device):
        pltpu.make_async_remote_copy(
            src_ref=src,
            dst_ref=dst,
            send_sem=pair[0],
            recv_sem=pair[1],
            device_id=device,
            device_id_type=MESH,
        ).start()

    def bytes_of(view, sem):
        return lambda: pltpu.make_async_copy(view, view, sem).wait()

    def all_but_self(buf, sem, own):
        def wait():
            @pl.when(own)
            def _():
                bytes_of(buf.at[pl.ds(0, buf.shape[0] - 1)], sem)()

            @pl.when(jnp.logical_not(own))
            def _():
                bytes_of(buf, sem)()

        return wait

    def cols(at, size):
        return pl.ds(pl.multiple_of(at, 128), size)

    krow = cols(core * 128, 128)
    mine = cols((4 * yy + xx) * PIECE, PIECE)
    owned = cols((4 * j + xx) * PIECE, PIECE)
    block = cols(xx * PIECE, PIECE)

    local("hid", r.hidden_in, r.hid_v)

    barrier = pltpu.get_barrier_semaphore()

    def greet(d, z):
        @pl.when(jnp.logical_not((d == i) & (z == j)))
        def _():
            pl.semaphore_signal(barrier, inc=1, device_id=(d, z), device_id_type=MESH)

    def greet_far(k, _):
        greet(2 * k + core, yy)
        greet(8 * yy + 2 * lax.rem(k, 4) + core, lax.div(k, 4))
        return 0

    def greet_plane(k, _):
        greet(k, j)
        return 0

    lax.fori_loop(0, CHIPS, greet_far, 0)
    lax.fori_loop(0, NDP, greet_plane, 0)

    local("rg", r.rec_gain.at[:, mine], r.rgain_v.at[0])
    local("rg1", r.rec_gain.at[:, owned], r.rgain_v.at[1])
    merged = []
    for l in range(LAYERS):
        for q in range(2):
            merged.append((("in", l), r.rec_in_x.at[l], r.wi.at[l], q, 2 * q * PIECE, PIECE))
            merged.append((("in", l), r.rec_in_y.at[l], r.wi.at[l], q, (2 * q + 1) * PIECE, PIECE))
        merged.append((("out", l), r.rec_out.at[l], r.wr.at[l], 0, 0, HALF))
    merged.append((("q",), r.attn_q, r.wq, 0, 0, HALF))
    merged.append((("o",), r.attn_out, r.wo, 0, 0, HALF))

    def weight_part(src, q, size, c):
        return src.at[:, cols(c * HALF + q * size, size)]

    for n, (tag, src, dst, q, at, size) in enumerate(merged):
        local(("own", *tag, n), weight_part(src, q, size, core), dst.at[krow, pl.ds(at, size)])
    local("cw", r.conv_weight.at[:, :, block], r.cw_v)
    local("cb", r.conv_bias.at[:, block], r.cb_v)
    local("gxb", r.gate_x_bias.at[:, block], r.gxb_v)
    local("gab", r.gate_a_bias.at[:, block], r.gab_v)
    local("dec", r.decay_param.at[:, block], r.dec_v)
    local("gxw", r.gate_x_weight.at[:, xx], r.gxw_v)
    local("gaw", r.gate_a_weight.at[:, xx], r.gaw_v)
    local("sc", r.scale_index, r.scale_s)
    local("pos", r.positions, r.pos_s)
    local("win", r.conv_state, r.win_v)
    local("ag", r.attn_gain.at[:, owned], r.again_v)
    local("wkv", r.attn_kv, r.wkv_v)
    local("key", r.key_cache, r.key_v)
    local("val", r.value_cache, r.val_v)

    late3 = lax.broadcasted_iota(jnp.int32, (NX, ROWS, PIECE), 1) >= SEQ

    def turned(values):
        return pltpu.roll(values, SEQ, 1)

    lane = lax.broadcasted_iota(jnp.int32, (BLOCK, 128), 1)
    diag = lane == lax.broadcasted_iota(jnp.int32, (BLOCK, 128), 0)

    def norm_line(k, line):
        me = NX * j + xx
        r.nsend[k] = line
        r.nbuf[k, me] = line
        pair = sems()

        def one(n, _):
            x, z = lax.div(n, NMP), lax.rem(n, NMP)

            @pl.when(jnp.logical_not((x == xx) & (z == j)))
            def _():
                remote(r.nsend.at[k], r.nbuf.at[k, me], pair, (8 * yy + 2 * x + core, z))

            return 0

        lax.fori_loop(0, CHIPS, one, 0)
        view = r.nbuf.at[k, pl.ds(0, CHIPS - 1)]
        pending["norm", k] = bytes_of(view, pair[1])
        pending["norm sent", k] = bytes_of(view, pair[0])

    def norm_first():
        h = r.h_v[...]
        sq = jnp.broadcast_to(jnp.sum(h * h, axis=-1, keepdims=True), (ROWS, 128))
        here = lax.broadcasted_iota(jnp.int32, (ROWS, 128), 1) - 8 * xx
        at = here == lax.broadcasted_iota(jnp.int32, (ROWS, 128), 0)
        line = jnp.sum(jnp.where(at, sq, 0.0), axis=0, keepdims=True)
        norm_line(0, line)

    def norm_send(k):
        x = r.x_v[...]
        sq = jnp.sum((x * x).reshape(BLOCK, PIECE), axis=-1, keepdims=True)
        norm_line(k, jnp.sum(jnp.where(diag, jnp.broadcast_to(sq, (BLOCK, 128)), 0.0), axis=0, keepdims=True))

    def norm_scale(k):
        take(("norm", k))
        total = r.nbuf[k, 0]
        for n in range(1, CHIPS):
            total = total + r.nbuf[k, n]
        line = lax.rsqrt(total * (1.0 / 4096.0) + 1e-06)
        return jnp.sum(jnp.where(diag, jnp.broadcast_to(line, (BLOCK, 128)), 0.0), axis=-1, keepdims=True)

    def half_sent(name, half, pair):
        pending[name] = all_but_self(half, pair[1], diagonal)
        pending[name + " sent"] = all_but_self(half, pair[0], diagonal)

    def spread(k):
        pair = sems()
        me = lax.div(i, 2)

        def one(n, _):
            q = lax.div(n, NMP)
            z = lax.rem(n, NMP)
            d = 8 * j + 2 * q + core

            @pl.when(jnp.logical_not((d == i) & (z == j)))
            def _():
                remote(r.pieces.at[k, q], r.spread_b.at[k, core, me], pair, (d, z))

            return 0

        lax.fori_loop(0, CHIPS, one, 0)
        half_sent(f"spread{k}", r.spread_b.at[k, core], pair)

        @pl.when(diagonal)
        def _():
            r.spread_b[k, core, me] = r.pieces[k, xx]

    def gather(k):
        pair = sems()

        def one(z, _):
            d = 8 * j + 2 * xx + core

            @pl.when(jnp.logical_not((d == i) & (z == j)))
            def _():
                remote(r.act_s.at[k], r.act_b.at[k, core, yy], pair, (d, z))

            return 0

        lax.fori_loop(0, NMP, one, 0)
        half_sent(f"gather{k}", r.act_b.at[k, core], pair)

        @pl.when(diagonal)
        def _():
            r.act_b[k, core, yy] = r.act_s[k]

    def halves(name, buf):
        own = buf.at[core]
        take(name)
        pair = sems()
        remote(own, own, pair, (mate, j))
        pending[name + " on"] = bytes_of(own, pair[0])
        yield core, own
        bytes_of(own, pair[1])()
        yield 1 - core, buf.at[1 - core]

    def gathered(k):
        for c, part in halves(f"gather{k}", r.act_b.at[k]):
            yield c, part[...].reshape(4 * BLOCK, PIECE)

    def spread_in(k, gain):
        for c, part in halves(f"spread{k}", r.spread_b.at[k]):
            act = part[...].astype(F32).reshape(4 * BLOCK, PIECE)
            yield c, (act if gain is None else act * gain).astype(BF16)

    def reduce_start(name, buf):
        pair = sems()
        pending[name] = all_but_self(buf, pair[1], inside)
        pending[name + " sent"] = all_but_self(buf, pair[0], inside)
        return pair

    def reduce(pair, send, buf, c):
        me = NX * yy + xx

        def one(n, _):
            q, at = lax.div(n, 4), lax.rem(n + yy + 2, 4)
            d = 8 * at + 2 * (2 * core + q) + c

            @pl.when(d != i)
            def _():
                remote(send.at[q, 4 * c + at], buf.at[me], pair, (d, j))

            return 0

        lax.fori_loop(0, BLOCKS, one, 0)

    def reduce_own(send, buf):
        @pl.when(inside)
        def _():
            buf[NX * yy + xx] = send[xx - 2 * core, 4 * core + yy]

    def total_of(buf, at):
        acc = buf[0, :, at].astype(F32)
        for n in range(1, CHIPS):
            acc = acc + buf[n, :, at].astype(F32)
        return acc

    def reduce_all_start(name, buf):
        pair = sems()
        view = buf.at[pl.ds(0, NDP - 1)]
        pending[name] = bytes_of(view, pair[1])
        pending[name + " sent"] = bytes_of(view, pair[0])
        return pair

    def reduce_all(pair, send, buf, c):
        def one(n, _):
            d = 2 * lax.rem(lax.div(i, 2) + 8 + n, CHIPS) + c

            @pl.when(d != i)
            def _():
                remote(send.at[row_slot(d)], buf.at[i], pair, (d, j))

            return 0

        lax.fori_loop(0, CHIPS, one, 0)

    def reduce_all_own(send, buf):
        buf[i] = send[row_slot(i)]

    def summed(buf, c, at):
        acc = buf[c, :, at].astype(F32)
        for p in range(1, NDP // 2):
            acc = acc + buf[2 * p + c, :, at].astype(F32)
        return acc

    def row_slot(d):
        return CHIPS * lax.rem(d, 2) + lax.div(d, 2)

    take("hid")
    r.h_v[0:SEQ, :] = r.hid_v[0].astype(F32)
    r.h_v[SEQ:ROWS, :] = r.hid_v[1].astype(F32)
    for q in range(NMP):
        r.pieces[0, q] = r.h_v[:, q * PIECE : (q + 1) * PIECE].astype(BF16)

    met = 2 * CHIPS - 1 + NDP - 1
    pl.semaphore_wait(barrier, jnp.where(diagonal, met - 1, met))
    spread(0)

    def trade(tag):
        pair = sems()
        total = 0
        for t, src, dst, q, at, size in merged:
            if t == tag:
                remote(weight_part(src, q, size, 1 - core), dst.at[krow, pl.ds(at, size)], pair, (mate, j))
                total += size
        for t, src, dst, q, at, size in merged:
            if t == tag:
                whole = dst.at[krow, pl.ds(0, total)]
        pending["mate", *tag] = bytes_of(whole, pair[1])
        pending["mate sent", *tag] = bytes_of(whole, pair[0])

    def merged_ready(tag):
        for n, (t, *_) in enumerate(merged):
            if t == tag:
                take(("own", *tag, n))
        take(("mate", *tag))

    def states_send():
        pairs = sems(), sems(), sems()

        def one(n, _):
            x = lax.rem(xx + n, NX)
            device = (8 * yy + 2 * x + core, j)
            remote(r.pieces.at[0, x], r.ent_b.at[xx], pairs[2], device)
            remote(r.lru_state.at[:, :, cols(x * PIECE, PIECE)], r.lru_b.at[xx], pairs[0], device)
            remote(r.conv_state.at[:, :, :, cols(x * PIECE, PIECE)], r.win_b.at[xx], pairs[1], device)
            return 0

        lax.fori_loop(1, NX, one, 0)
        local("lru own", r.lru_state.at[:, :, block], r.lru_b.at[xx])
        local("win own", r.conv_state.at[:, :, :, block], r.win_b.at[xx])
        r.ent_b[xx] = r.pieces[0, xx]
        for name, buf, pair in (
            ("lru", r.lru_b, pairs[0]),
            ("window", r.win_b, pairs[1]),
            ("entering", r.ent_b, pairs[2]),
        ):
            view = buf.at[pl.ds(0, NX - 1)]
            pending[name] = bytes_of(view, pair[1])
            pending[name + " sent"] = bytes_of(view, pair[0])

    trade(("in", 0))
    norm_first()
    states_send()
    trade(("out", 0))
    trade(("in", 1))
    trade(("out", 1))
    trade(("q",))
    trade(("o",))

    scales = []

    def prepare():
        take("pos")
        srow = lax.broadcasted_iota(jnp.int32, (ROWS, SLOTS), 0)
        slot = lax.broadcasted_iota(jnp.int32, (ROWS, SLOTS), 1) + j * SLOTS
        seq = srow & 3
        pos = jnp.where(
            seq == 0,
            r.pos_s[0],
            jnp.where(seq == 1, r.pos_s[1], jnp.where(seq == 2, r.pos_s[2], r.pos_s[3])),
        )
        step = lax.shift_right_logical(srow, 2)
        held = pos - 1 - ((pos - 1 - slot) & (WIN - 1))
        r.mask_v[...] = jnp.where((held >= 0) & (held >= pos + step - (WIN - 1)), 1.0, 0.0).astype(F32)
        take("win")
        for l in range(LAYERS):
            r.conv_out[l, 0] = r.win_v[l, 2]
        take("sc", "lru", "lru own", "window", "win own")
        for l in range(LAYERS):
            power = (r.scale_s[l].astype(F32) - 4.0) * 0.5
            scales.append(jnp.exp2(jnp.full((1, 128), power, F32))[:, :1])
            for x in range(NX):
                r.st_v[l, x, 0:SEQ, :] = r.lru_b[x, l].astype(F32) * scales[l]
                r.st_v[l, x, SEQ:ROWS, :] = jnp.zeros((SEQ, PIECE), F32)
                w0 = r.win_b[x, l, 0].astype(F32)
                w1 = r.win_b[x, l, 1].astype(F32)
                w2 = r.win_b[x, l, 2].astype(F32)
                r.t0_v[l, x, 0:SEQ, :] = w0
                r.t0_v[l, x, SEQ:ROWS, :] = w1
                r.t1_v[l, x, 0:SEQ, :] = w1
                r.t1_v[l, x, SEQ:ROWS, :] = w2
                r.t2_v[l, x, 0:SEQ, :] = w2
                r.t2_v[l, x, SEQ:ROWS, :] = jnp.zeros((SEQ, PIECE), F32)
        take("cw", "cb", "gxb", "gab", "dec", "gxw", "gaw", "rg1", "entering")
        r.x_v[...] = r.ent_b[...].astype(F32)

    def give_back(l):
        pairs = sems(), sems()

        def one(n, _):
            x = lax.rem(xx + n, NX)
            device = (8 * yy + 2 * x + core, j)
            remote(r.lru_s.at[l, x], r.lru_out.at[l, :, block], pairs[0], device)
            remote(r.win_s.at[l, x], r.conv_out.at[l, pl.ds(1, 2), :, block], pairs[1], device)
            return 0

        lax.fori_loop(1, NX, one, 0)
        r.lru_out[l, :, block] = r.lru_s[l, xx]
        r.conv_out[l, 1:3, :, block] = r.win_s[l, xx]
        for name, buf, pair in (("lru", r.lru_s, pairs[0]), ("window", r.win_s, pairs[1])):
            view = buf.at[l, pl.ds(0, NX - 1)]
            pending[name + " back", l] = bytes_of(view, pair[1])
            pending[name + " back sent", l] = bytes_of(view, pair[0])

    def recurrent(l, parts, meanwhile):
        pair = reduce_start(f"in{l}", r.in_b.at[l])
        for c, act in parts:
            for n in range(4):
                part = jnp.dot(act, r.wi[l, :, n * PIECE : (n + 1) * PIECE], preferred_element_type=F32)
                at = slice((n % 2) * PIECE, (n % 2 + 1) * PIECE)
                r.in_s[l, n // 2, pl.ds(4 * c, 4), :, at] = part.reshape(4, BLOCK, PIECE).astype(BF16)
            reduce(pair, r.in_s.at[l], r.in_b.at[l], c)
        reduce_own(r.in_s.at[l], r.in_b.at[l])
        meanwhile()
        decay = r.dec_v[l : l + 1, :]
        soft = jnp.maximum(decay, 0.0) + jnp.log1p(jnp.exp(-jnp.abs(decay)))
        soft = soft.reshape(1, 1, PIECE)

        def tap(n):
            return r.cw_v[l, n : n + 1, :].reshape(1, 1, PIECE)

        bias = r.cb_v[l : l + 1, :].reshape(1, 1, PIECE)
        early = tap(0) * r.t0_v[l] + tap(1) * r.t1_v[l] + bias
        scale = norm_scale(l)
        take(f"in{l}")
        u = (total_of(r.in_b.at[l], slice(0, PIECE)) * scale).astype(BF16).astype(F32)
        u = u.reshape(NX, ROWS, PIECE)
        v = (total_of(r.in_b.at[l], slice(PIECE, HALF)) * scale).reshape(NX, ROWS, PIECE)
        u_turned = turned(u)
        t2 = jnp.where(late3, u_turned, r.t2_v[l])
        filtered = early + tap(2) * t2 + tap(3) * u
        half = filtered.reshape(BLOCK, PIECE).astype(BF16)
        gx = jnp.dot(half, r.gxw_v[l], preferred_element_type=F32) + r.gxb_v[l : l + 1, :]
        ga = jnp.dot(half, r.gaw_v[l], preferred_element_type=F32) + r.gab_v[l : l + 1, :]
        gx = (1.0 / (1.0 + jnp.exp(-gx))).reshape(NX, ROWS, PIECE)
        ga = (1.0 / (1.0 + jnp.exp(-ga))).reshape(NX, ROWS, PIECE)
        log_a = -8.0 * ga * soft
        a = jnp.exp(log_a)
        add = jnp.sqrt(1.0 - jnp.exp(2.0 * log_a)) * (gx * filtered)
        first = a * r.st_v[l] + add
        second = a * turned(first) + add
        state = jnp.where(late3, second, first)
        gelu = 0.5 * v * (1.0 + jnp.tanh(0.7978845608028654 * (v + 0.044715 * (v * v * v))))
        r.act_s[2 * l] = (state * gelu).reshape(BLOCK, PIECE).astype(BF16)
        gather(2 * l)
        state_turned = turned(state)
        for x in range(NX):
            r.lru_s[l, x] = (state_turned[x, 0:SEQ] / scales[l]).astype(BF16)
            r.win_s[l, x, 0] = u[x, 0:SEQ].astype(BF16)
            r.win_s[l, x, 1] = u_turned[x, 0:SEQ].astype(BF16)
        give_back(l)

        merged_ready(("out", l))
        pair = reduce_start(f"out{l}", r.out_b.at[l])
        for c, act in gathered(2 * l):
            for n in range(2):
                part = jnp.dot(act, r.wr[l, :, n * PIECE : (n + 1) * PIECE], preferred_element_type=F32)
                r.out_s[l, n, pl.ds(4 * c, 4)] = part.reshape(4, BLOCK, PIECE).astype(BF16)
            reduce(pair, r.out_s.at[l], r.out_b.at[l], c)
        reduce_own(r.out_s.at[l], r.out_b.at[l])
        take(f"out{l}")
        r.x_v[...] = r.x_v[...] + total_of(r.out_b.at[l], slice(0, PIECE)).reshape(NX, ROWS, PIECE)

    def next_act(k, gain):
        r.act_s[k] = (r.x_v[...].reshape(BLOCK, PIECE) * gain).astype(BF16)
        gather(k)

    merged_ready(("in", 0))
    take("rg")
    recurrent(0, spread_in(0, r.rgain_v[0, 0:1, :]), prepare)
    next_act(1, r.rgain_v[1, 1:2, :])
    norm_send(1)
    merged_ready(("in", 1))
    recurrent(1, gathered(1), lambda: None)
    take("ag")
    next_act(3, r.again_v[...])
    norm_send(2)

    pair = sems()
    r.res_s[...] = r.x_v[...]

    def stream_send(n, _):
        x = lax.rem(xx + n, NX)
        remote(r.res_s.at[x], r.res_b.at[xx], pair, (8 * yy + 2 * x + core, j))
        return 0

    lax.fori_loop(1, NX, stream_send, 0)
    r.res_b[xx] = r.res_s[xx]
    view = r.res_b.at[pl.ds(0, NX - 1)]
    pending["stream"] = bytes_of(view, pair[1])
    pending["stream sent"] = bytes_of(view, pair[0])

    take("wkv", "key", "val")
    merged_ready(("q",))
    pair = reduce_all_start("q", r.q_b)
    for c, act in gathered(3):
        rows = pl.ds(CHIPS * c, CHIPS)
        for n in range(2):
            at = slice(n * PIECE, (n + 1) * PIECE)
            part = jnp.dot(act, r.wq[:, at], preferred_element_type=F32)
            r.q_s[rows, :, at] = part.reshape(CHIPS, ROWS, PIECE).astype(BF16)
        act = r.act_b[3, c, :, :, krow].reshape(4 * BLOCK, 128)
        part = jnp.dot(act, r.wkv_v[...], preferred_element_type=F32)
        r.q_s[rows, :, HALF:] = part.reshape(CHIPS, ROWS, 128).astype(BF16)
        reduce_all(pair, r.q_s, r.q_b, c)
    reduce_all_own(r.q_s, r.q_b)
    scale = norm_scale(2)
    own = jnp.zeros((ROWS, 1), F32)
    for x in range(NX):
        own = jnp.where(xx == x, scale[x * ROWS : (x + 1) * ROWS], own)
    scale = own
    take("q")
    for c in range(2):
        at = slice(c * HALF, (c + 1) * HALF)
        r.zsend[:, at] = (summed(r.q_b, c, slice(0, HALF)) * scale).astype(BF16)
    at = slice(HALF, HALF + 128)
    kv = (summed(r.q_b, 0, at) + summed(r.q_b, 1, at)) * scale
    r.zsend[:, FEAT:] = kv.astype(BF16)
    query_pair, part_pair, top_pair = sems(), sems(), sems()

    def query_send(d, _):
        remote(r.zsend, r.zbuf.at[j], query_pair, (i, lax.rem(j + d, NMP)))
        return 0

    lax.fori_loop(1, NMP, query_send, 0)
    view = r.zbuf.at[pl.ds(0, NMP - 1)]
    pending["query"] = bytes_of(view, query_pair[1])
    pending["query sent"] = bytes_of(view, query_pair[0])
    r.zbuf[j] = r.zsend[...]
    r.new_kv[0] = kv[0:SEQ].astype(BF16)
    r.new_kv[1] = pltpu.roll(kv, SEQ, 0)[0:SEQ].astype(BF16)
    take("query")

    rows = HEADS * ROWS
    query = jnp.concatenate(
        [
            r.zbuf[z, :, h * HEAD_DIM : (h + 1) * HEAD_DIM].astype(F32)
            for z in range(NMP)
            for h in range(HEADS // NMP)
        ],
        axis=0,
    ).astype(BF16)
    which = lax.broadcasted_iota(jnp.int32, (rows, SLOTS), 0) & 3
    scores = None
    for b in range(SEQ):
        one = lax.dot_general(
            query, r.key_v[b], (((1,), (1,)), ((), ())), preferred_element_type=F32
        )
        scores = one if scores is None else jnp.where(which == b, one, scores)
    mask = jnp.broadcast_to(r.mask_v[...][None], (HEADS, ROWS, SLOTS)).reshape(rows, SLOTS)
    scores = jnp.where(mask > 0.5, scores * HEAD_DIM ** (-0.5), -1e30)
    top = jnp.max(scores, axis=-1, keepdims=True)
    weight = jnp.exp(scores - top) * mask
    total = jnp.sum(weight, axis=-1, keepdims=True)
    values = None
    for b in range(SEQ):
        one = jnp.dot(
            jnp.where(which == b, weight, 0.0).astype(BF16), r.val_v[b], preferred_element_type=F32
        )
        values = one if values is None else values + one
    lane = lax.broadcasted_iota(jnp.int32, (rows, 128), 1)
    r.csend[...] = values.reshape(HEADS, ROWS, HEAD_DIM).astype(BF16)
    r.tsend[...] = jnp.where(lane < 64, top, total).reshape(HEADS, ROWS, 128)

    def part_send(d, _):
        z = lax.rem(j + d, NMP)
        group = pl.ds(4 * z, 4)
        remote(r.csend.at[group], r.cbuf.at[j], part_pair, (i, z))
        remote(r.tsend.at[group], r.tbuf.at[j], top_pair, (i, z))
        return 0

    lax.fori_loop(1, NMP, part_send, 0)
    for name, buf, pair in (("part", r.cbuf, part_pair), ("top", r.tbuf, top_pair)):
        view = buf.at[pl.ds(0, NMP - 1)]
        pending[name] = bytes_of(view, pair[1])
        pending[name + " sent"] = bytes_of(view, pair[0])
    r.cbuf[j] = r.csend[pl.ds(4 * j, 4)]
    r.tbuf[j] = r.tsend[pl.ds(4 * j, 4)]

    lateh = lax.broadcasted_iota(jnp.int32, (ROWS, HEAD_DIM), 0) >= SEQ
    late1 = lax.broadcasted_iota(jnp.int32, (ROWS, 1), 0) >= SEQ

    def pair(lo, hi):
        at = slice(FEAT, FEAT + 128)
        both = jnp.concatenate([r.zbuf[lo, :, at].astype(F32), r.zbuf[hi, :, at].astype(F32)], axis=1)
        turned = pltpu.roll(both, SEQ, 0)
        return jnp.where(lateh, turned, both), jnp.where(lateh, both, turned)

    key0, key1 = pair(0, 1)
    val0, val1 = pair(2, 3)
    fresh = []
    for h in range(4):
        head = r.zsend[:, h * HEAD_DIM : (h + 1) * HEAD_DIM].astype(F32)
        s0 = jnp.sum(head * key0, axis=-1, keepdims=True) * HEAD_DIM ** (-0.5)
        s1 = jnp.sum(head * key1, axis=-1, keepdims=True) * HEAD_DIM ** (-0.5)
        fresh.append((s0, jnp.where(late1, s1, -1e30)))
    take("part", "top")
    for h in range(4):
        s0, s1 = fresh[h]
        tops = [r.tbuf[z, h, :, 0:1] for z in range(NMP)]
        best = jnp.maximum(s0, s1)
        for t in tops:
            best = jnp.maximum(best, t)
        w0 = jnp.exp(s0 - best)
        w1 = jnp.where(late1, jnp.exp(s1 - best), 0.0)
        den = w0 + w1
        num = w0.astype(BF16).astype(F32) * val0 + w1.astype(BF16).astype(F32) * val1
        for z in range(NMP):
            fade = jnp.exp(tops[z] - best)
            den = den + fade * r.tbuf[z, h, :, 64:65]
            num = num + fade * r.cbuf[z, h].astype(F32)
        r.pieces[1, h] = (num / den).astype(BF16)
    spread(1)
    merged_ready(("o",))
    pair = reduce_all_start("o", r.o_b)
    for c, act in spread_in(1, None):
        for n in range(2):
            at = slice(n * PIECE, (n + 1) * PIECE)
            part = jnp.dot(act, r.wo[:, at], preferred_element_type=F32)
            r.o_s[pl.ds(CHIPS * c, CHIPS), :, at] = part.reshape(CHIPS, ROWS, PIECE).astype(BF16)
        reduce_all(pair, r.o_s, r.o_b, c)
    reduce_all_own(r.o_s, r.o_b)
    take("stream", "o")
    for q in range(NMP):
        at = slice((q % 2) * PIECE, (q % 2 + 1) * PIECE)
        x = r.res_b[q] + summed(r.o_b, q // 2, at)
        at = slice(q * PIECE, (q + 1) * PIECE)
        r.hidden_out[0, :, at] = x[0:SEQ].astype(BF16)
        r.hidden_out[1, :, at] = pltpu.roll(x, SEQ, 0)[0:SEQ].astype(BF16)

    take(*list(pending))


def hand_over(*refs):
    for src, dst in zip(refs[:4], refs[4:]):
        dst[...] = src[...]


def body(*args):
    args = list(args)
    args[15] = args[15].reshape(1, -1)
    shape = jax.ShapeDtypeStruct
    hbm = pl.BlockSpec(memory_space=pltpu.HBM)
    vmem = pl.BlockSpec(memory_space=pltpu.VMEM)
    outs = pl.pallas_call(
        kernel,
        out_shape=(
            shape((STEPS, SEQ, FEAT), BF16),
            shape((LAYERS, SEQ, FEAT), BF16),
            shape((LAYERS, 3, SEQ, FEAT), BF16),
            shape((STEPS, SEQ, 128), BF16),
        ),
        in_specs=[hbm] * 22,
        out_specs=(vmem,) * 4,
        scratch_shapes=[kind for _, kind in scratch_list()],
        compiler_params=pltpu.CompilerParams(
            collective_id=0, has_side_effects=True, vmem_limit_bytes=VMEM
        ),
    )(*args)
    return pl.pallas_call(
        hand_over,
        out_shape=tuple(shape(out.shape, out.dtype) for out in outs),
        in_specs=[vmem] * 4,
        out_specs=(vmem,) * 4,
    )(*outs)


def solution(mesh):
    placed = (
        P(None, "dp", "mp"),
        P(),
        P(None, "dp", "mp"),
        P(None, "dp", "mp"),
        P(None, None, "mp"),
        P(None, "mp"),
        P(None, "mp", None, None),
        P(None, "mp"),
        P(None, "mp", None, None),
        P(None, "mp"),
        P(None, "mp"),
        P(None, "dp", "mp"),
        P(None, "dp", "mp"),
        P(None, None, "dp", "mp"),
        P(),
        P(),
        P("dp", "mp"),
        P("dp", "mp"),
        P("dp", "mp"),
        P("dp", "mp", None),
        P("dp", "mp", None),
        P("dp"),
    )
    return jax.shard_map(
        body,
        mesh=mesh,
        in_specs=placed,
        out_specs=(
            P(None, "dp", "mp"),
            P(None, "dp", "mp"),
            P(None, None, "dp", "mp"),
            P(None, "dp", "mp"),
        ),
        check_vma=False,
    )
```

time: 506 us -> 99.1 us (0.20)
  waiting for transfers between devices: 225 us -> 0 us
  starting transfers between devices: 118 us -> 0 us
  Pallas kernels: 0 us -> 97.3 us
  blocking collectives: 83.9 us -> 0 us
  local copies, waits for them, and re-layouts: 41.5 us -> 0 us
  other arithmetic: 19.1 us -> 0 us
  matrix products: 11.1 us -> 0 us
    all_to_all x29 -> x0, waiting for transfers between devices: 225 us -> none  [the longest x12 136 us: sent_and_summed(): lax.all_to_all(cut_along(array, dim, devices), axis, 0, 0, tiled=True)]
    all_to_all x29 -> x0, starting transfers between devices: 118 us -> none  [the longest x12 51.1 us: sent_and_summed(): lax.all_to_all(cut_along(array, dim, devices), axis, 0, 0, tiled=True)]
    pallas_call x0 -> x2, Pallas kernels: none -> 97.3 us  [the longest x1 95.8 us: body(): pl.pallas_call(kernel, out_shape=(shape((STEPS, SEQ, FEAT), BF16), shape(...]
    all_to_all x9 -> x0, blocking collectives: 83.9 us -> none  [the longest x4 43.3 us: spread_project(): lax.all_to_all(normed, 'dp', split_axis=1, concat_axis=0, tiled=True)]
    dot_general x12 -> x0, local copies, waits for them, and re-layouts: 15.9 us -> none  [spread_project(): jnp.dot(spread, weight, preferred_element_type=jnp.float32)]
    dot_general x27 -> x0, matrix products: 11.1 us -> none  [the longest x12 7.68 us: spread_project(): jnp.dot(spread, weight, preferred_element_type=jnp.float32)]
    unnamed x170 -> x0, local copies, waits for them, and re-layouts: 10 us -> none
    reduce_sum x23 -> x0, other arithmetic: 8.62 us -> none  [the longest x12 7.23 us: sent_and_summed(): return jnp.sum(pieces, axis=0)]
  transfers between devices with their start and end apart: 29 -> 0, of which waited for: 29 -> 0; matrix products, arithmetic and copies ran while one was open for 8% -> 0% of each run, Pallas kernels for 0% -> 0%
where the time goes in v2:
time: 99.1 us; the launch traced here: 97.9 us
  Pallas kernels  97.3 us (98%)
    pallas_call x1, Pallas kernels, body(): pl.pallas_call(kernel, out_shape=(shape((STEPS, SEQ, FEAT), BF16), shape(...  95.8 us

profile of v2, /device:TPU:0, one launch (start us, length us, event | category | flops | bytes accessed | tf_op | source)
XLA Modules:
  0.0 97.9 jit_solution(13759121264389036835)
XLA Ops:
  0.6 95.8 %shard_map.237 = (bf16[2,4,1024]{2,1,0:T(4,128)(2,1)}, bf16[2,4,1024]{2,1,0:T(4,128)(2,1)}, bf16[2,3,4,1024]{3,2,1,0:T(4,128)(2,1)}, bf16[2,4,128]{2,1,0:T(4,128)(2,1)}) custom-call(bf16[2,4,1024]{2,1,0:T(4,128)(2,1)} %refs_0_.1, f32[2,4096]{1,0:T(2,128)} %refs_1_.1, bf16[2,128,1024]{2,1,0:T(8,128)(2,1)} %refs_2_.1, bf16[2,128,1024]{2,1,0:T(8,128)(2,1)} %refs_3_.1, ...), custom_call_target="tpu_custom_call" | custom-call | tf_op jit(solution)/shard_map/pallas_call | solution.py:781
  96.4 1.5 %shard_map.238 = (bf16[2,4,1024]{2,1,0:T(4,128)(2,1)}, bf16[2,4,1024]{2,1,0:T(4,128)(2,1)}, bf16[2,3,4,1024]{3,2,1,0:T(4,128)(2,1)}, bf16[2,4,128]{2,1,0:T(4,128)(2,1)}) custom-call(bf16[2,4,1024]{2,1,0:T(4,128)(2,1)} %get-tuple-element.8.refs_0_, bf16[2,4,1024]{2,1,0:T(4,128)(2,1)} %get-tuple-element.9.refs_1_, ...), custom_call_target="tpu_custom_call" | custom-call | tf_op jit(solution)/shard_map/pallas_call | solution.py:796

commit v3 on v2

--- a/solution.py
+++ b/solution.py
@@ -46,11 +46,11 @@
         ("win_v", V((LAYERS, 3, SEQ, FEAT), BF16)),
         ("key_v", V((SEQ, SLOTS, HEAD_DIM), BF16)),
         ("val_v", V((SEQ, SLOTS, HEAD_DIM), BF16)),
-        ("wkv_v", V((128, 128), BF16)),
-        ("wi", V((LAYERS, PIECE, 2 * HALF), BF16)),
-        ("wr", V((LAYERS, PIECE, HALF), BF16)),
-        ("wq", V((PIECE, HALF), BF16)),
-        ("wo", V((PIECE, HALF), BF16)),
+        ("wkv", V((PIECE, 128), BF16)),
+        ("wi", V((LAYERS, PIECE, 2 * FEAT), BF16)),
+        ("wr", V((LAYERS, PIECE, FEAT), BF16)),
+        ("wq", V((PIECE, FEAT), BF16)),
+        ("wo", V((PIECE, FEAT), BF16)),
         ("scale_s", pltpu.SMEM((LAYERS,), jnp.int32)),
         ("pos_s", pltpu.SMEM((SEQ,), jnp.int32)),
         ("x_v", V((NX, ROWS, PIECE), F32)),
@@ -65,17 +65,17 @@
         ("lru_s", V((LAYERS, NX, SEQ, PIECE), BF16)),
         ("win_s", V((LAYERS, NX, 2, SEQ, PIECE), BF16)),
         ("pieces", V((2, NMP, ROWS, PIECE), BF16)),
-        ("spread_b", V((2, 2, CHIPS, ROWS, PIECE), BF16)),
+        ("spread_b", V((2, CHIPS, ROWS, PIECE), BF16)),
         ("act_s", V((4, BLOCK, PIECE), BF16)),
-        ("act_b", V((4, 2, 4, BLOCK, PIECE), BF16)),
-        ("in_s", V((LAYERS, 2, BLOCKS, BLOCK, HALF), BF16)),
+        ("act_b", V((4, 4, BLOCK, PIECE), BF16)),
+        ("in_s", V((LAYERS, NX, 4, BLOCK, HALF), BF16)),
         ("in_b", V((LAYERS, CHIPS, BLOCK, HALF), BF16)),
-        ("out_s", V((LAYERS, 2, BLOCKS, BLOCK, PIECE), BF16)),
+        ("out_s", V((LAYERS, NX, 4, BLOCK, PIECE), BF16)),
         ("out_b", V((LAYERS, CHIPS, BLOCK, PIECE), BF16)),
-        ("q_s", V((NDP, ROWS, HALF + 128), BF16)),
-        ("q_b", V((NDP, ROWS, HALF + 128), BF16)),
-        ("o_s", V((NDP, ROWS, HALF), BF16)),
-        ("o_b", V((NDP, ROWS, HALF), BF16)),
+        ("q_s", V((CHIPS, ROWS, FEAT + 128), BF16)),
+        ("q_b", V((CHIPS, ROWS, FEAT + 128), BF16)),
+        ("o_s", V((CHIPS, ROWS, FEAT), BF16)),
+        ("o_b", V((CHIPS, ROWS, FEAT), BF16)),
         ("ent_b", V((NX, ROWS, PIECE), BF16)),
         ("res_s", V((NX, ROWS, PIECE), F32)),
         ("res_b", V((NX, ROWS, PIECE), F32)),
@@ -139,7 +139,7 @@
     yy = lax.div(i, 8)
     xx = lax.div(lax.rem(i, 8), 2)
     diagonal = yy == j
-    inside = lax.div(xx, 2) == core
+    place = lax.div(i, 2)
 
     pending = {}
     used = [0, 0]
@@ -202,34 +202,27 @@
         def _():
             pl.semaphore_signal(barrier, inc=1, device_id=(d, z), device_id_type=MESH)
 
-    def greet_far(k, _):
+    def greet_all(k, _):
         greet(2 * k + core, yy)
+        greet(2 * k + core, j)
         greet(8 * yy + 2 * lax.rem(k, 4) + core, lax.div(k, 4))
         return 0
 
-    def greet_plane(k, _):
-        greet(k, j)
-        return 0
-
-    lax.fori_loop(0, CHIPS, greet_far, 0)
-    lax.fori_loop(0, NDP, greet_plane, 0)
+    lax.fori_loop(0, CHIPS, greet_all, 0)
+    greet(mate, j)
 
     local("rg", r.rec_gain.at[:, mine], r.rgain_v.at[0])
     local("rg1", r.rec_gain.at[:, owned], r.rgain_v.at[1])
     merged = []
     for l in range(LAYERS):
-        for q in range(2):
-            merged.append((("in", l), r.rec_in_x.at[l], r.wi.at[l], q, 2 * q * PIECE, PIECE))
-            merged.append((("in", l), r.rec_in_y.at[l], r.wi.at[l], q, (2 * q + 1) * PIECE, PIECE))
-        merged.append((("out", l), r.rec_out.at[l], r.wr.at[l], 0, 0, HALF))
-    merged.append((("q",), r.attn_q, r.wq, 0, 0, HALF))
-    merged.append((("o",), r.attn_out, r.wo, 0, 0, HALF))
-
-    def weight_part(src, q, size, c):
-        return src.at[:, cols(c * HALF + q * size, size)]
-
-    for n, (tag, src, dst, q, at, size) in enumerate(merged):
-        local(("own", *tag, n), weight_part(src, q, size, core), dst.at[krow, pl.ds(at, size)])
+        merged.append((("in", l), r.rec_in_x.at[l], r.wi.at[l, krow, pl.ds(0, FEAT)]))
+        merged.append((("in", l), r.rec_in_y.at[l], r.wi.at[l, krow, pl.ds(FEAT, FEAT)]))
+        merged.append((("out", l), r.rec_out.at[l], r.wr.at[l, krow, :]))
+    merged.append((("q",), r.attn_q, r.wq.at[krow, :]))
+    merged.append((("q",), r.attn_kv, r.wkv.at[krow, :]))
+    merged.append((("o",), r.attn_out, r.wo.at[krow, :]))
+    for n, (tag, src, dst) in enumerate(merged):
+        local(("own", n), src, dst)
     local("cw", r.conv_weight.at[:, :, block], r.cw_v)
     local("cb", r.conv_bias.at[:, block], r.cb_v)
     local("gxb", r.gate_x_bias.at[:, block], r.gxb_v)
@@ -241,7 +234,6 @@
     local("pos", r.positions, r.pos_s)
     local("win", r.conv_state, r.win_v)
     local("ag", r.attn_gain.at[:, owned], r.again_v)
-    local("wkv", r.attn_kv, r.wkv_v)
     local("key", r.key_cache, r.key_v)
     local("val", r.value_cache, r.val_v)
 
@@ -294,95 +286,92 @@
         line = lax.rsqrt(total * (1.0 / 4096.0) + 1e-06)
         return jnp.sum(jnp.where(diag, jnp.broadcast_to(line, (BLOCK, 128)), 0.0), axis=-1, keepdims=True)
 
-    def half_sent(name, half, pair):
-        pending[name] = all_but_self(half, pair[1], diagonal)
-        pending[name + " sent"] = all_but_self(half, pair[0], diagonal)
-
     def spread(k):
         pair = sems()
-        me = lax.div(i, 2)
 
         def one(n, _):
             q = lax.div(n, NMP)
-            z = lax.rem(n, NMP)
+            z = lax.rem(n + j + 2, NMP)
             d = 8 * j + 2 * q + core
 
             @pl.when(jnp.logical_not((d == i) & (z == j)))
             def _():
-                remote(r.pieces.at[k, q], r.spread_b.at[k, core, me], pair, (d, z))
+                remote(r.pieces.at[k, q], r.spread_b.at[k, place], pair, (d, z))
 
             return 0
 
         lax.fori_loop(0, CHIPS, one, 0)
-        half_sent(f"spread{k}", r.spread_b.at[k, core], pair)
+        pending["spread", k] = all_but_self(r.spread_b.at[k], pair[1], diagonal)
+        pending["spread sent", k] = all_but_self(r.spread_b.at[k], pair[0], diagonal)
 
         @pl.when(diagonal)
         def _():
-            r.spread_b[k, core, me] = r.pieces[k, xx]
+            r.spread_b[k, place] = r.pieces[k, xx]
 
     def gather(k):
         pair = sems()
 
-        def one(z, _):
+        def one(n, _):
+            z = lax.rem(n + j + 2, NMP)
             d = 8 * j + 2 * xx + core
 
             @pl.when(jnp.logical_not((d == i) & (z == j)))
             def _():
-                remote(r.act_s.at[k], r.act_b.at[k, core, yy], pair, (d, z))
+                remote(r.act_s.at[k], r.act_b.at[k, yy], pair, (d, z))
 
             return 0
 
         lax.fori_loop(0, NMP, one, 0)
-        half_sent(f"gather{k}", r.act_b.at[k, core], pair)
+        pending["gather", k] = all_but_self(r.act_b.at[k], pair[1], diagonal)
+        pending["gather sent", k] = all_but_self(r.act_b.at[k], pair[0], diagonal)
 
         @pl.when(diagonal)
         def _():
-            r.act_b[k, core, yy] = r.act_s[k]
-
-    def halves(name, buf):
-        own = buf.at[core]
-        take(name)
+            r.act_b[k, yy] = r.act_s[k]
+
+    def gathered(k):
+        take(("gather", k))
+        return r.act_b[k].reshape(4 * BLOCK, PIECE)
+
+    def spread_in(k):
+        take(("spread", k))
+        return r.spread_b[k].astype(F32).reshape(4 * BLOCK, PIECE)
+
+    def others(name, buf):
         pair = sems()
-        remote(own, own, pair, (mate, j))
-        pending[name + " on"] = bytes_of(own, pair[0])
-        yield core, own
-        bytes_of(own, pair[1])()
-        yield 1 - core, buf.at[1 - core]
-
-    def gathered(k):
-        for c, part in halves(f"gather{k}", r.act_b.at[k]):
-            yield c, part[...].reshape(4 * BLOCK, PIECE)
-
-    def spread_in(k, gain):
-        for c, part in halves(f"spread{k}", r.spread_b.at[k]):
-            act = part[...].astype(F32).reshape(4 * BLOCK, PIECE)
-            yield c, (act if gain is None else act * gain).astype(BF16)
-
-    def reduce_start(name, buf):
-        pair = sems()
-        pending[name] = all_but_self(buf, pair[1], inside)
-        pending[name + " sent"] = all_but_self(buf, pair[0], inside)
+        view = buf.at[pl.ds(0, CHIPS - 1)]
+        pending[name] = bytes_of(view, pair[1])
+        pending[name + " sent"] = bytes_of(view, pair[0])
         return pair
 
-    def reduce(pair, send, buf, c):
-        me = NX * yy + xx
-
+    def column(n):
+        return lax.rem(xx + (2, 1, 3, 0)[n], NX)
+
+    def reduce(pair, send, buf, q):
         def one(n, _):
-            q, at = lax.div(n, 4), lax.rem(n + yy + 2, 4)
-            d = 8 * at + 2 * (2 * core + q) + c
+            at = lax.rem(n + yy + 2, 4)
+            d = 8 * at + 2 * q + core
 
             @pl.when(d != i)
             def _():
-                remote(send.at[q, 4 * c + at], buf.at[me], pair, (d, j))
+                remote(send.at[q, at], buf.at[place], pair, (d, j))
 
             return 0
 
-        lax.fori_loop(0, BLOCKS, one, 0)
-
-    def reduce_own(send, buf):
-        @pl.when(inside)
-        def _():
-            buf[NX * yy + xx] = send[xx - 2 * core, 4 * core + yy]
+        lax.fori_loop(0, 4, one, 0)
+
+    def reduce_all(pair, send, buf):
+        def one(n, _):
+            to = lax.rem(place + 8 + n, CHIPS)
+
+            @pl.when(to != place)
+            def _():
+                remote(send.at[to], buf.at[place], pair, (2 * to + core, j))
+
+            return 0
+
+        lax.fori_loop(0, CHIPS, one, 0)
+        buf[place] = send[place]
 
     def total_of(buf, at):
         acc = buf[0, :, at].astype(F32)
@@ -390,36 +379,11 @@
             acc = acc + buf[n, :, at].astype(F32)
         return acc
 
-    def reduce_all_start(name, buf):
-        pair = sems()
-        view = buf.at[pl.ds(0, NDP - 1)]
-        pending[name] = bytes_of(view, pair[1])
-        pending[name + " sent"] = bytes_of(view, pair[0])
-        return pair
-
-    def reduce_all(pair, send, buf, c):
-        def one(n, _):
-            d = 2 * lax.rem(lax.div(i, 2) + 8 + n, CHIPS) + c
-
-            @pl.when(d != i)
-            def _():
-                remote(send.at[row_slot(d)], buf.at[i], pair, (d, j))
-
-            return 0
-
-        lax.fori_loop(0, CHIPS, one, 0)
-
-    def reduce_all_own(send, buf):
-        buf[i] = send[row_slot(i)]
-
-    def summed(buf, c, at):
-        acc = buf[c, :, at].astype(F32)
-        for p in range(1, NDP // 2):
-            acc = acc + buf[2 * p + c, :, at].astype(F32)
+    def summed(buf, at):
+        acc = buf[0, :, at].astype(F32)
+        for p in range(1, CHIPS):
+            acc = acc + buf[p, :, at].astype(F32)
         return acc
-
-    def row_slot(d):
-        return CHIPS * lax.rem(d, 2) + lax.div(d, 2)
 
     take("hid")
     r.h_v[0:SEQ, :] = r.hid_v[0].astype(F32)
@@ -427,28 +391,21 @@
     for q in range(NMP):
         r.pieces[0, q] = r.h_v[:, q * PIECE : (q + 1) * PIECE].astype(BF16)
 
-    met = 2 * CHIPS - 1 + NDP - 1
+    met = 3 * CHIPS - 1
     pl.semaphore_wait(barrier, jnp.where(diagonal, met - 1, met))
     spread(0)
 
-    def trade(tag):
-        pair = sems()
-        total = 0
-        for t, src, dst, q, at, size in merged:
-            if t == tag:
-                remote(weight_part(src, q, size, 1 - core), dst.at[krow, pl.ds(at, size)], pair, (mate, j))
-                total += size
-        for t, src, dst, q, at, size in merged:
-            if t == tag:
-                whole = dst.at[krow, pl.ds(0, total)]
-        pending["mate", *tag] = bytes_of(whole, pair[1])
-        pending["mate sent", *tag] = bytes_of(whole, pair[0])
+    def trade():
+        for n, (_, src, dst) in enumerate(merged):
+            pair = sems()
+            remote(src, dst, pair, (mate, j))
+            pending["mate", n] = bytes_of(dst, pair[1])
+            pending["mate sent", n] = bytes_of(dst, pair[0])
 
     def merged_ready(tag):
         for n, (t, *_) in enumerate(merged):
             if t == tag:
-                take(("own", *tag, n))
-        take(("mate", *tag))
+                take(("own", n), ("mate", n))
 
     def states_send():
         pairs = sems(), sems(), sems()
@@ -474,14 +431,9 @@
             pending[name] = bytes_of(view, pair[1])
             pending[name + " sent"] = bytes_of(view, pair[0])
 
-    trade(("in", 0))
+    trade()
     norm_first()
     states_send()
-    trade(("out", 0))
-    trade(("in", 1))
-    trade(("out", 1))
-    trade(("q",))
-    trade(("o",))
 
     scales = []
 
@@ -538,15 +490,17 @@
             pending[name + " back", l] = bytes_of(view, pair[1])
             pending[name + " back sent", l] = bytes_of(view, pair[0])
 
-    def recurrent(l, parts, meanwhile):
-        pair = reduce_start(f"in{l}", r.in_b.at[l])
-        for c, act in parts:
-            for n in range(4):
-                part = jnp.dot(act, r.wi[l, :, n * PIECE : (n + 1) * PIECE], preferred_element_type=F32)
-                at = slice((n % 2) * PIECE, (n % 2 + 1) * PIECE)
-                r.in_s[l, n // 2, pl.ds(4 * c, 4), :, at] = part.reshape(4, BLOCK, PIECE).astype(BF16)
-            reduce(pair, r.in_s.at[l], r.in_b.at[l], c)
-        reduce_own(r.in_s.at[l], r.in_b.at[l])
+    def recurrent(l, act, meanwhile):
+        pair = others(f"in{l}", r.in_b.at[l])
+        for n in range(NX):
+            q = column(n)
+            for side in range(2):
+                weight = r.wi[l, :, cols(side * FEAT + q * PIECE, PIECE)]
+                part = jnp.dot(act, weight, preferred_element_type=F32)
+                at = slice(side * PIECE, (side + 1) * PIECE)
+                r.in_s[l, q, :, :, at] = part.reshape(4, BLOCK, PIECE).astype(BF16)
+            reduce(pair, r.in_s.at[l], r.in_b.at[l], q)
+        r.in_b[l, place] = r.in_s[l, xx, yy]
         meanwhile()
         decay = r.dec_v[l : l + 1, :]
         soft = jnp.maximum(decay, 0.0) + jnp.log1p(jnp.exp(-jnp.abs(decay)))
@@ -587,13 +541,14 @@
         give_back(l)
 
         merged_ready(("out", l))
-        pair = reduce_start(f"out{l}", r.out_b.at[l])
-        for c, act in gathered(2 * l):
-            for n in range(2):
-                part = jnp.dot(act, r.wr[l, :, n * PIECE : (n + 1) * PIECE], preferred_element_type=F32)
-                r.out_s[l, n, pl.ds(4 * c, 4)] = part.reshape(4, BLOCK, PIECE).astype(BF16)
-            reduce(pair, r.out_s.at[l], r.out_b.at[l], c)
-        reduce_own(r.out_s.at[l], r.out_b.at[l])
+        act = gathered(2 * l)
+        pair = others(f"out{l}", r.out_b.at[l])
+        for n in range(NX):
+            q = column(n)
+            part = jnp.dot(act, r.wr[l, :, cols(q * PIECE, PIECE)], preferred_element_type=F32)
+            r.out_s[l, q] = part.reshape(4, BLOCK, PIECE).astype(BF16)
+            reduce(pair, r.out_s.at[l], r.out_b.at[l], q)
+        r.out_b[l, place] = r.out_s[l, xx, yy]
         take(f"out{l}")
         r.x_v[...] = r.x_v[...] + total_of(r.out_b.at[l], slice(0, PIECE)).reshape(NX, ROWS, PIECE)
 
@@ -603,7 +558,7 @@
 
     merged_ready(("in", 0))
     take("rg")
-    recurrent(0, spread_in(0, r.rgain_v[0, 0:1, :]), prepare)
+    recurrent(0, (spread_in(0) * r.rgain_v[0, 0:1, :]).astype(BF16), prepare)
     next_act(1, r.rgain_v[1, 1:2, :])
     norm_send(1)
     merged_ready(("in", 1))
@@ -626,31 +581,25 @@
     pending["stream"] = bytes_of(view, pair[1])
     pending["stream sent"] = bytes_of(view, pair[0])
 
-    take("wkv", "key", "val")
+    take("key", "val")
     merged_ready(("q",))
-    pair = reduce_all_start("q", r.q_b)
-    for c, act in gathered(3):
-        rows = pl.ds(CHIPS * c, CHIPS)
-        for n in range(2):
-            at = slice(n * PIECE, (n + 1) * PIECE)
-            part = jnp.dot(act, r.wq[:, at], preferred_element_type=F32)
-            r.q_s[rows, :, at] = part.reshape(CHIPS, ROWS, PIECE).astype(BF16)
-        act = r.act_b[3, c, :, :, krow].reshape(4 * BLOCK, 128)
-        part = jnp.dot(act, r.wkv_v[...], preferred_element_type=F32)
-        r.q_s[rows, :, HALF:] = part.reshape(CHIPS, ROWS, 128).astype(BF16)
-        reduce_all(pair, r.q_s, r.q_b, c)
-    reduce_all_own(r.q_s, r.q_b)
+    act = gathered(3)
+    pair = others("q", r.q_b)
+    for n in range(4):
+        at = slice(n * PIECE, (n + 1) * PIECE)
+        part = jnp.dot(act, r.wq[:, at], preferred_element_type=F32)
+        r.q_s[:, :, at] = part.reshape(CHIPS, ROWS, PIECE).astype(BF16)
+    part = jnp.dot(act, r.wkv[...], preferred_element_type=F32)
+    r.q_s[:, :, FEAT:] = part.reshape(CHIPS, ROWS, 128).astype(BF16)
+    reduce_all(pair, r.q_s, r.q_b)
     scale = norm_scale(2)
     own = jnp.zeros((ROWS, 1), F32)
     for x in range(NX):
         own = jnp.where(xx == x, scale[x * ROWS : (x + 1) * ROWS], own)
     scale = own
     take("q")
-    for c in range(2):
-        at = slice(c * HALF, (c + 1) * HALF)
-        r.zsend[:, at] = (summed(r.q_b, c, slice(0, HALF)) * scale).astype(BF16)
-    at = slice(HALF, HALF + 128)
-    kv = (summed(r.q_b, 0, at) + summed(r.q_b, 1, at)) * scale
+    r.zsend[:, 0:FEAT] = (summed(r.q_b, slice(0, FEAT)) * scale).astype(BF16)
+    kv = summed(r.q_b, slice(FEAT, FEAT + 128)) * scale
     r.zsend[:, FEAT:] = kv.astype(BF16)
     query_pair, part_pair, top_pair = sems(), sems(), sems()
 
@@ -748,19 +697,17 @@
         r.pieces[1, h] = (num / den).astype(BF16)
     spread(1)
     merged_ready(("o",))
-    pair = reduce_all_start("o", r.o_b)
-    for c, act in spread_in(1, None):
-        for n in range(2):
-            at = slice(n * PIECE, (n + 1) * PIECE)
-            part = jnp.dot(act, r.wo[:, at], preferred_element_type=F32)
-            r.o_s[pl.ds(CHIPS * c, CHIPS), :, at] = part.reshape(CHIPS, ROWS, PIECE).astype(BF16)
-        reduce_all(pair, r.o_s, r.o_b, c)
-    reduce_all_own(r.o_s, r.o_b)
+    act = spread_in(1).astype(BF16)
+    pair = others("o", r.o_b)
+    for n in range(4):
+        at = slice(n * PIECE, (n + 1) * PIECE)
+        part = jnp.dot(act, r.wo[:, at], preferred_element_type=F32)
+        r.o_s[:, :, at] = part.reshape(CHIPS, ROWS, PIECE).astype(BF16)
+    reduce_all(pair, r.o_s, r.o_b)
     take("stream", "o")
     for q in range(NMP):
-        at = slice((q % 2) * PIECE, (q % 2 + 1) * PIECE)
-        x = r.res_b[q] + summed(r.o_b, q // 2, at)
         at = slice(q * PIECE, (q + 1) * PIECE)
+        x = r.res_b[q] + summed(r.o_b, at)
         r.hidden_out[0, :, at] = x[0:SEQ].astype(BF16)
         r.hidden_out[1, :, at] = pltpu.roll(x, SEQ, 0)[0:SEQ].astype(BF16)
 

time: 99.1 us -> 93.7 us (0.946); the launches traced: 97.9 us -> 93.5 us
  Pallas kernels: 97.3 us -> 92.9 us
    pallas_call x1, Pallas kernels: 95.8 us -> 91.4 us  [body(): pl.pallas_call(kernel, out_shape=(shape((STEPS, SEQ, FEAT), BF16), shape(...]
where the time goes in v3:
time: 93.7 us; the launch traced here: 93.5 us
  Pallas kernels  92.9 us (99%)
    pallas_call x1, Pallas kernels, body(): pl.pallas_call(kernel, out_shape=(shape((STEPS, SEQ, FEAT), BF16), shape(...  91.4 us

profile of v3, /device:TPU:0, one launch (start us, length us, event | category | flops | bytes accessed | tf_op | source)
XLA Modules:
  0.0 93.5 jit_solution(15070002758550306150)
XLA Ops:
  0.6 91.4 %shard_map.237 = (bf16[2,4,1024]{2,1,0:T(4,128)(2,1)}, bf16[2,4,1024]{2,1,0:T(4,128)(2,1)}, bf16[2,3,4,1024]{3,2,1,0:T(4,128)(2,1)}, bf16[2,4,128]{2,1,0:T(4,128)(2,1)}) custom-call(bf16[2,4,1024]{2,1,0:T(4,128)(2,1)} %refs_0_.1, f32[2,4096]{1,0:T(2,128)} %refs_1_.1, bf16[2,128,1024]{2,1,0:T(8,128)(2,1)} %refs_2_.1, bf16[2,128,1024]{2,1,0:T(8,128)(2,1)} %refs_3_.1, ...), custom_call_target="tpu_custom_call" | custom-call | tf_op jit(solution)/shard_map/pallas_call | solution.py:728
  92.0 1.5 %shard_map.238 = (bf16[2,4,1024]{2,1,0:T(4,128)(2,1)}, bf16[2,4,1024]{2,1,0:T(4,128)(2,1)}, bf16[2,3,4,1024]{3,2,1,0:T(4,128)(2,1)}, bf16[2,4,128]{2,1,0:T(4,128)(2,1)}) custom-call(bf16[2,4,1024]{2,1,0:T(4,128)(2,1)} %get-tuple-element.8.refs_0_, bf16[2,4,1024]{2,1,0:T(4,128)(2,1)} %get-tuple-element.9.refs_1_, ...), custom_call_target="tpu_custom_call" | custom-call | tf_op jit(solution)/shard_map/pallas_call | solution.py:743

commit v4 on v3

--- a/solution.py
+++ b/solution.py
@@ -185,6 +185,9 @@
 
         return wait
 
+    def away(here, n):
+        return lax.rem(here + (2, 1, 3, 0)[n], 4)
+
     def cols(at, size):
         return pl.ds(pl.multiple_of(at, 128), size)
 
@@ -208,7 +211,7 @@
         greet(8 * yy + 2 * lax.rem(k, 4) + core, lax.div(k, 4))
         return 0
 
-    lax.fori_loop(0, CHIPS, greet_all, 0)
+    lax.fori_loop(0, CHIPS, greet_all, 0, unroll=True)
     greet(mate, j)
 
     local("rg", r.rec_gain.at[:, mine], r.rgain_v.at[0])
@@ -260,7 +263,7 @@
 
             return 0
 
-        lax.fori_loop(0, CHIPS, one, 0)
+        lax.fori_loop(0, CHIPS, one, 0, unroll=True)
         view = r.nbuf.at[k, pl.ds(0, CHIPS - 1)]
         pending["norm", k] = bytes_of(view, pair[1])
         pending["norm sent", k] = bytes_of(view, pair[0])
@@ -289,18 +292,14 @@
     def spread(k):
         pair = sems()
 
-        def one(n, _):
-            q = lax.div(n, NMP)
-            z = lax.rem(n + j + 2, NMP)
+        for n in range(CHIPS):
+            q, z = away(xx, n // 4), away(j, n % 4)
             d = 8 * j + 2 * q + core
 
             @pl.when(jnp.logical_not((d == i) & (z == j)))
             def _():
                 remote(r.pieces.at[k, q], r.spread_b.at[k, place], pair, (d, z))
 
-            return 0
-
-        lax.fori_loop(0, CHIPS, one, 0)
         pending["spread", k] = all_but_self(r.spread_b.at[k], pair[1], diagonal)
         pending["spread sent", k] = all_but_self(r.spread_b.at[k], pair[0], diagonal)
 
@@ -311,17 +310,14 @@
     def gather(k):
         pair = sems()
 
-        def one(n, _):
-            z = lax.rem(n + j + 2, NMP)
+        for n in range(NMP):
+            z = away(j, n)
             d = 8 * j + 2 * xx + core
 
             @pl.when(jnp.logical_not((d == i) & (z == j)))
             def _():
                 remote(r.act_s.at[k], r.act_b.at[k, yy], pair, (d, z))
 
-            return 0
-
-        lax.fori_loop(0, NMP, one, 0)
         pending["gather", k] = all_but_self(r.act_b.at[k], pair[1], diagonal)
         pending["gather sent", k] = all_but_self(r.act_b.at[k], pair[0], diagonal)
 
@@ -345,32 +341,20 @@
         return pair
 
     def column(n):
-        return lax.rem(xx + (2, 1, 3, 0)[n], NX)
-
-    def reduce(pair, send, buf, q):
-        def one(n, _):
-            at = lax.rem(n + yy + 2, 4)
+        return away(xx, n)
+
+    def reduce(pair, send, buf, q, last):
+        for n in range(4):
+            at = away(yy, n)
             d = 8 * at + 2 * q + core
 
-            @pl.when(d != i)
-            def _():
+            if not (last and n == 3):
                 remote(send.at[q, at], buf.at[place], pair, (d, j))
 
-            return 0
-
-        lax.fori_loop(0, 4, one, 0)
-
     def reduce_all(pair, send, buf):
-        def one(n, _):
-            to = lax.rem(place + 8 + n, CHIPS)
-
-            @pl.when(to != place)
-            def _():
-                remote(send.at[to], buf.at[place], pair, (2 * to + core, j))
-
-            return 0
-
-        lax.fori_loop(0, CHIPS, one, 0)
+        for n in range(CHIPS - 1):
+            to = 4 * away(yy, n // 4) + away(xx, n % 4)
+            remote(send.at[to], buf.at[place], pair, (2 * to + core, j))
         buf[place] = send[place]
 
     def total_of(buf, at):
@@ -418,7 +402,7 @@
             remote(r.conv_state.at[:, :, :, cols(x * PIECE, PIECE)], r.win_b.at[xx], pairs[1], device)
             return 0
 
-        lax.fori_loop(1, NX, one, 0)
+        lax.fori_loop(1, NX, one, 0, unroll=True)
         local("lru own", r.lru_state.at[:, :, block], r.lru_b.at[xx])
         local("win own", r.conv_state.at[:, :, :, block], r.win_b.at[xx])
         r.ent_b[xx] = r.pieces[0, xx]
@@ -482,7 +466,7 @@
             remote(r.win_s.at[l, x], r.conv_out.at[l, pl.ds(1, 2), :, block], pairs[1], device)
             return 0
 
-        lax.fori_loop(1, NX, one, 0)
+        lax.fori_loop(1, NX, one, 0, unroll=True)
         r.lru_out[l, :, block] = r.lru_s[l, xx]
         r.conv_out[l, 1:3, :, block] = r.win_s[l, xx]
         for name, buf, pair in (("lru", r.lru_s, pairs[0]), ("window", r.win_s, pairs[1])):
@@ -499,7 +483,7 @@
                 part = jnp.dot(act, weight, preferred_element_type=F32)
                 at = slice(side * PIECE, (side + 1) * PIECE)
                 r.in_s[l, q, :, :, at] = part.reshape(4, BLOCK, PIECE).astype(BF16)
-            reduce(pair, r.in_s.at[l], r.in_b.at[l], q)
+            reduce(pair, r.in_s.at[l], r.in_b.at[l], q, n == NX - 1)
         r.in_b[l, place] = r.in_s[l, xx, yy]
         meanwhile()
         decay = r.dec_v[l : l + 1, :]
@@ -547,7 +531,7 @@
             q = column(n)
             part = jnp.dot(act, r.wr[l, :, cols(q * PIECE, PIECE)], preferred_element_type=F32)
             r.out_s[l, q] = part.reshape(4, BLOCK, PIECE).astype(BF16)
-            reduce(pair, r.out_s.at[l], r.out_b.at[l], q)
+            reduce(pair, r.out_s.at[l], r.out_b.at[l], q, n == NX - 1)
         r.out_b[l, place] = r.out_s[l, xx, yy]
         take(f"out{l}")
         r.x_v[...] = r.x_v[...] + total_of(r.out_b.at[l], slice(0, PIECE)).reshape(NX, ROWS, PIECE)
@@ -556,9 +540,10 @@
         r.act_s[k] = (r.x_v[...].reshape(BLOCK, PIECE) * gain).astype(BF16)
         gather(k)
 
+    prepare()
     merged_ready(("in", 0))
     take("rg")
-    recurrent(0, (spread_in(0) * r.rgain_v[0, 0:1, :]).astype(BF16), prepare)
+    recurrent(0, (spread_in(0) * r.rgain_v[0, 0:1, :]).astype(BF16), lambda: None)
     next_act(1, r.rgain_v[1, 1:2, :])
     norm_send(1)
     merged_ready(("in", 1))
@@ -575,7 +560,7 @@
         remote(r.res_s.at[x], r.res_b.at[xx], pair, (8 * yy + 2 * x + core, j))
         return 0
 
-    lax.fori_loop(1, NX, stream_send, 0)
+    lax.fori_loop(1, NX, stream_send, 0, unroll=True)
     r.res_b[xx] = r.res_s[xx]
     view = r.res_b.at[pl.ds(0, NX - 1)]
     pending["stream"] = bytes_of(view, pair[1])
@@ -607,7 +592,7 @@
         remote(r.zsend, r.zbuf.at[j], query_pair, (i, lax.rem(j + d, NMP)))
         return 0
 
-    lax.fori_loop(1, NMP, query_send, 0)
+    lax.fori_loop(1, NMP, query_send, 0, unroll=True)
     view = r.zbuf.at[pl.ds(0, NMP - 1)]
     pending["query"] = bytes_of(view, query_pair[1])
     pending["query sent"] = bytes_of(view, query_pair[0])
@@ -654,7 +639,7 @@
         remote(r.tsend.at[group], r.tbuf.at[j], top_pair, (i, z))
         return 0
 
-    lax.fori_loop(1, NMP, part_send, 0)
+    lax.fori_loop(1, NMP, part_send, 0, unroll=True)
     for name, buf, pair in (("part", r.cbuf, part_pair), ("top", r.tbuf, top_pair)):
         view = buf.at[pl.ds(0, NMP - 1)]
         pending[name] = bytes_of(view, pair[1])

time: 93.7 us -> 89.8 us (0.958)
  Pallas kernels: 92.9 us -> 89 us
    pallas_call x1, Pallas kernels: 91.4 us -> 87.5 us  [body(): pl.pallas_call(kernel, out_shape=(shape((STEPS, SEQ, FEAT), BF16), shape(...]
where the time goes in v4:
time: 89.8 us; the launch traced here: 89.6 us
  Pallas kernels  89 us (99%)
    pallas_call x1, Pallas kernels, body(): pl.pallas_call(kernel, out_shape=(shape((STEPS, SEQ, FEAT), BF16), shape(...  87.5 us

profile of v4, /device:TPU:0, one launch (start us, length us, event | category | flops | bytes accessed | tf_op | source)
XLA Modules:
  0.0 89.6 jit_solution(18030635684955913002)
XLA Ops:
  0.6 87.5 %shard_map.237 = (bf16[2,4,1024]{2,1,0:T(4,128)(2,1)}, bf16[2,4,1024]{2,1,0:T(4,128)(2,1)}, bf16[2,3,4,1024]{3,2,1,0:T(4,128)(2,1)}, bf16[2,4,128]{2,1,0:T(4,128)(2,1)}) custom-call(bf16[2,4,1024]{2,1,0:T(4,128)(2,1)} %refs_0_.1, f32[2,4096]{1,0:T(2,128)} %refs_1_.1, bf16[2,128,1024]{2,1,0:T(8,128)(2,1)} %refs_2_.1, bf16[2,128,1024]{2,1,0:T(8,128)(2,1)} %refs_3_.1, ...), custom_call_target="tpu_custom_call" | custom-call | tf_op jit(solution)/shard_map/pallas_call | solution.py:713
  88.2 1.5 %shard_map.238 = (bf16[2,4,1024]{2,1,0:T(4,128)(2,1)}, bf16[2,4,1024]{2,1,0:T(4,128)(2,1)}, bf16[2,3,4,1024]{3,2,1,0:T(4,128)(2,1)}, bf16[2,4,128]{2,1,0:T(4,128)(2,1)}) custom-call(bf16[2,4,1024]{2,1,0:T(4,128)(2,1)} %get-tuple-element.8.refs_0_, bf16[2,4,1024]{2,1,0:T(4,128)(2,1)} %get-tuple-element.9.refs_1_, ...), custom_call_target="tpu_custom_call" | custom-call | tf_op jit(solution)/shard_map/pallas_call | solution.py:728

commit v5 on v4

--- a/solution.py
+++ b/solution.py
@@ -26,6 +26,7 @@
 BLOCKS = 8
 BLOCK = 32
 CHIPS = 16
+ORDER = sorted(range(16), key=lambda n: -((2, 1, 1, 0)[n // 4] + (2, 1, 1, 0)[n % 4]))
 VMEM = 67043328
 
 
@@ -201,17 +202,21 @@
     barrier = pltpu.get_barrier_semaphore()
 
     def greet(d, z):
-        @pl.when(jnp.logical_not((d == i) & (z == j)))
-        def _():
-            pl.semaphore_signal(barrier, inc=1, device_id=(d, z), device_id_type=MESH)
-
-    def greet_all(k, _):
-        greet(2 * k + core, yy)
-        greet(2 * k + core, j)
-        greet(8 * yy + 2 * lax.rem(k, 4) + core, lax.div(k, 4))
-        return 0
-
-    lax.fori_loop(0, CHIPS, greet_all, 0, unroll=True)
+        pl.semaphore_signal(barrier, inc=1, device_id=(d, z), device_id_type=MESH)
+
+    for n in range(CHIPS):
+        d = 8 * away(yy, n // 4) + 2 * away(xx, n % 4) + core
+        if n < CHIPS - 1:
+            greet(d, yy)
+        else:
+
+            @pl.when(jnp.logical_not(diagonal))
+            def _():
+                greet(d, yy)
+
+    for n in range(CHIPS - 1):
+        greet(8 * yy + 2 * away(xx, n % 4) + core, away(j, n // 4))
+        greet(8 * away(yy, n // 4) + 2 * away(xx, n % 4) + core, j)
     greet(mate, j)
 
     local("rg", r.rec_gain.at[:, mine], r.rgain_v.at[0])
@@ -352,7 +357,7 @@
                 remote(send.at[q, at], buf.at[place], pair, (d, j))
 
     def reduce_all(pair, send, buf):
-        for n in range(CHIPS - 1):
+        for n in ORDER[: CHIPS - 1]:
             to = 4 * away(yy, n // 4) + away(xx, n % 4)
             remote(send.at[to], buf.at[place], pair, (2 * to + core, j))
         buf[place] = send[place]

time: 89.8 us -> 89.9 us (level)
  no operation moved by 1% of the time
where the time goes in v5:
time: 89.9 us; the launch traced here: 89.7 us
  Pallas kernels  89 us (99%)
    pallas_call x1, Pallas kernels, body(): pl.pallas_call(kernel, out_shape=(shape((STEPS, SEQ, FEAT), BF16), shape(...  87.6 us

profile of v5, /device:TPU:0, one launch (start us, length us, event | category | flops | bytes accessed | tf_op | source)
XLA Modules:
  0.0 89.7 jit_solution(738745068344733558)
XLA Ops:
  0.6 87.6 %shard_map.237 = (bf16[2,4,1024]{2,1,0:T(4,128)(2,1)}, bf16[2,4,1024]{2,1,0:T(4,128)(2,1)}, bf16[2,3,4,1024]{3,2,1,0:T(4,128)(2,1)}, bf16[2,4,128]{2,1,0:T(4,128)(2,1)}) custom-call(bf16[2,4,1024]{2,1,0:T(4,128)(2,1)} %refs_0_.1, f32[2,4096]{1,0:T(2,128)} %refs_1_.1, bf16[2,128,1024]{2,1,0:T(8,128)(2,1)} %refs_2_.1, bf16[2,128,1024]{2,1,0:T(8,128)(2,1)} %refs_3_.1, ...), custom_call_target="tpu_custom_call" | custom-call | tf_op jit(solution)/shard_map/pallas_call | solution.py:718
  88.2 1.5 %shard_map.238 = (bf16[2,4,1024]{2,1,0:T(4,128)(2,1)}, bf16[2,4,1024]{2,1,0:T(4,128)(2,1)}, bf16[2,3,4,1024]{3,2,1,0:T(4,128)(2,1)}, bf16[2,4,128]{2,1,0:T(4,128)(2,1)}) custom-call(bf16[2,4,1024]{2,1,0:T(4,128)(2,1)} %get-tuple-element.8.refs_0_, bf16[2,4,1024]{2,1,0:T(4,128)(2,1)} %get-tuple-element.9.refs_1_, ...), custom_call_target="tpu_custom_call" | custom-call | tf_op jit(solution)/shard_map/pallas_call | solution.py:733
